TPU v7x, 32 devices: a whole 2x2x4 slice. The times are simulated.
32 devices in a mesh: band: 8 (over z, y), mp: 4 (over x, core).
Axes of the slice: x: 2, y: 2, z: 4, core: 2. Of those that a mesh axis runs over, the one named last changes fastest.
Arguments:
- grid_latent: bfloat16 [32768, 512], P('band'), may hold values from -6 to 6
- edge_latent: bfloat16 [49152, 512], P('band'), may hold values from -6 to 6
- mesh_latent: bfloat16 [5120, 512], P('band', 'mp'), may hold values from -6 to 6
- mesh_grad: bfloat16 [5120, 512], P('band', 'mp'), may hold values from -96 to 96
- counts: int32 [5120], P('band'), may hold values from 8 to 64
- request: int32 [8, 7, 128], P('band'), may hold values from -1 to 639, as said below
- edge_sender: int32 [49152], P('band'), may hold values from 0 to 4095, as said below
- edge_slot: int32 [49152], P('band'), may hold values from 0 to 895, as said below
- w_send: bfloat16 [512, 512], P(None, 'mp'), may hold values from -0.25 to 0.25
- w_recv: bfloat16 [512, 512], P(None, 'mp'), may hold values from -0.25 to 0.25
- w_edge: bfloat16 [512, 512], P(None, 'mp'), may hold values from -0.25 to 0.25
- edge_bias: float32 [512], P('mp'), may hold values from -3 to 3
- w_out: bfloat16 [512, 512], P('mp'), may hold values from -0.25 to 0.25
Outputs:
- grid_grad: bfloat16 [32768, 512], P('band', 'mp')
- node_grad: bfloat16 [5120, 512], P('band', 'mp')
Inputs may be any that keep to these rules, and one draw needn't show every extreme that they name: request[p, k, c] is a node of patch p, numbered within the patch, wanted by band p + 3 - k, or -1 for an empty slot; where that band lies outside 0 to 7 all slots are -1; otherwise the live slots come first, name distinct nodes and number 1 or more; request[p, 3, c] is live for every c. `edge_sender`: within a band the senders never fall, and each grid point of the band sends one or two edges. edge_slot = k * 128 + c, the patch b + k - 3 of the edge's band b lies in 0 to 7, and request[b + k - 3, k, c] is never -1.
All inputs are finite; a program needn't handle non-finite values.
Results may differ from a plain program's by a relative error of at most 0.015.
Values may be sent and summed in bfloat16 or wider, within the bound.
A program may use at most 64 MiB of HBM per device.

v0:
```python
import jax
import jax.numpy as jnp
from jax import lax
from jax.sharding import PartitionSpec as P


def shifted(shard, axis, by):
    devices = lax.axis_size(axis)
    pairs = [(i, i + by) for i in range(devices) if 0 <= i + by < devices]
    return lax.ppermute(shard, axis, pairs)


def silu_slope(pre_act):
    sigmoid_value = jax.nn.sigmoid(pre_act)
    return sigmoid_value * (1.0 + pre_act * (1.0 - sigmoid_value))


def per_offset(blocks, reach, sign, mover):
    results = []
    for offset in range(blocks.shape[0]):
        amount = sign * (reach - offset)
        if amount == 0:
            results.append(blocks[offset])
        else:
            results.append(mover(blocks[offset], amount))
    return jnp.stack(results)


def split_pair(values):
    upper = values.astype(jnp.bfloat16)
    lower = (values - upper.astype(jnp.float32)).astype(jnp.bfloat16)
    return jnp.concatenate([upper, lower], axis=1)


def per_device(
    grid_latent,
    edge_latent,
    mesh_latent,
    mesh_grad,
    counts,
    request,
    edge_sender,
    edge_slot,
    w_send,
    w_recv,
    w_edge,
    edge_bias,
    w_out,
):
    span = request.shape[1]
    capacity = request.shape[2]
    reach = (span - 1) // 2
    node_count = mesh_latent.shape[0]
    grid_rows = grid_latent.shape[0]
    latent = grid_latent.shape[1]
    hidden_cols = w_send.shape[1]
    slot_count = span * capacity
    scaled_grad = (mesh_grad.astype(jnp.float32) / counts.astype(jnp.float32)[:, None]).astype(
        jnp.bfloat16
    )
    wanted = request[0]
    live_slot = (wanted >= 0)[:, :, None]
    picker = jnp.maximum(wanted, 0)
    flat_live = live_slot.reshape(slot_count, 1)
    flat_picker = picker.reshape(-1)
    send_both = jnp.stack(
        [
            jnp.where(live_slot, mesh_latent[picker], 0),
            jnp.where(live_slot, scaled_grad[picker], 0),
        ],
        axis=1,
    )
    got_part = per_offset(send_both, reach, 1, lambda block, amount: shifted(block, "band", amount))
    got = lax.all_gather(got_part, "mp", axis=3, tiled=True)
    slot_proj = jnp.dot(
        got[:, 0].reshape(slot_count, latent), w_recv, preferred_element_type=jnp.float32
    )
    slot_back = jnp.dot(
        got[:, 1].reshape(slot_count, latent), w_out.T, preferred_element_type=jnp.float32
    )
    edge_count = edge_sender.shape[0]
    width_rows = min(512, edge_count)
    block_count = -(-edge_count // width_rows)
    padding = block_count * width_rows - edge_count
    sender_pad = jnp.concatenate(
        [edge_sender, jnp.full((padding,), grid_rows + 2 * width_rows, jnp.int32)]
    )
    slot_pad = jnp.concatenate([edge_slot, jnp.full((padding,), -1, jnp.int32)])
    edge_pad = jnp.concatenate([edge_latent, jnp.zeros((padding, latent), edge_latent.dtype)])
    grid_proj = jnp.dot(grid_latent, w_send, preferred_element_type=jnp.float32)
    grid_split = split_pair(
        jnp.concatenate([grid_proj, jnp.zeros((width_rows, hidden_cols), jnp.float32)])
    )
    slot_split = split_pair(jnp.concatenate([slot_proj, slot_back], axis=1))
    window_iota = jnp.arange(width_rows, dtype=jnp.int32)
    slot_iota = jnp.arange(slot_count, dtype=jnp.int32)

    def one_block(carry, block_index):
        sender_acc, slot_acc = carry
        first_row = block_index * width_rows
        senders = lax.dynamic_slice_in_dim(sender_pad, first_row, width_rows, 0)
        slot_ids = lax.dynamic_slice_in_dim(slot_pad, first_row, width_rows, 0)
        edge_rows = lax.dynamic_slice_in_dim(edge_pad, first_row, width_rows, 0)
        anchor = senders[0]
        grid_pick = ((senders - anchor)[:, None] == window_iota[None, :]).astype(jnp.bfloat16)
        slot_pick = (slot_ids[:, None] == slot_iota[None, :]).astype(jnp.bfloat16)
        window = lax.dynamic_slice_in_dim(grid_split, anchor, width_rows, 0)
        grid_both = jnp.dot(grid_pick, window, preferred_element_type=jnp.float32)
        sender_proj = grid_both[:, :hidden_cols] + grid_both[:, hidden_cols:]
        slot_both = jnp.dot(slot_pick, slot_split, preferred_element_type=jnp.float32)
        recv_proj = slot_both[:, :hidden_cols] + slot_both[:, 2 * hidden_cols : 3 * hidden_cols]
        recv_back = slot_both[:, hidden_cols : 2 * hidden_cols] + slot_both[:, 3 * hidden_cols :]
        pre_act = sender_proj + recv_proj
        pre_act = (
            pre_act + jnp.dot(edge_rows, w_edge, preferred_element_type=jnp.float32) + edge_bias
        )
        edge_grad = (recv_back * silu_slope(pre_act)).astype(jnp.bfloat16)
        sender_part = lax.dot_general(
            grid_pick, edge_grad, (((0,), (0,)), ((), ())), preferred_element_type=jnp.float32
        )
        slot_part = lax.dot_general(
            slot_pick, edge_grad, (((0,), (0,)), ((), ())), preferred_element_type=jnp.float32
        )
        current = lax.dynamic_slice_in_dim(sender_acc, anchor, width_rows, 0)
        sender_acc = lax.dynamic_update_slice_in_dim(sender_acc, current + sender_part, anchor, 0)
        return ((sender_acc, slot_acc + slot_part), None)

    initial = (
        jnp.zeros((grid_rows + width_rows, hidden_cols), jnp.float32),
        jnp.zeros((slot_count, hidden_cols), jnp.float32),
    )
    (sender_acc, slot_sum), unused = lax.scan(
        one_block, initial, jnp.arange(block_count, dtype=jnp.int32)
    )
    sender_sum = sender_acc[:grid_rows].astype(jnp.bfloat16)
    recv_wide = w_recv.astype(jnp.float32)
    slot_term = jnp.dot(slot_sum, recv_wide.T, precision=lax.Precision.HIGHEST)
    slot_share = lax.psum_scatter(
        slot_term.astype(jnp.bfloat16), "mp", scatter_dimension=1, tiled=True
    ).astype(jnp.float32)
    part_cols = slot_share.shape[1]
    returned = per_offset(
        slot_share.reshape(span, capacity, part_cols),
        reach,
        -1,
        lambda block, amount: shifted(block.astype(jnp.bfloat16), "band", amount).astype(
            block.dtype
        ),
    )
    kept_rows = jnp.where(flat_live, returned.reshape(slot_count, part_cols), 0.0)
    node_grad = jax.ops.segment_sum(kept_rows, flat_picker, num_segments=node_count).astype(
        jnp.bfloat16
    )
    grid_term = jnp.dot(sender_sum, w_send.T, preferred_element_type=jnp.float32)
    grid_grad = lax.psum_scatter(
        grid_term.astype(jnp.bfloat16), "mp", scatter_dimension=1, tiled=True
    )
    return (grid_grad, node_grad)


def solution(mesh):
    in_specs = (
        P("band", None),
        P("band", None),
        P("band", "mp"),
        P("band", "mp"),
        P("band"),
        P("band", None, None),
        P("band"),
        P("band"),
        P(None, "mp"),
        P(None, "mp"),
        P(None, "mp"),
        P("mp"),
        P("mp", None),
    )
    out_specs = (P("band", "mp"), P("band", "mp"))
    return jax.shard_map(
        per_device, mesh=mesh, in_specs=in_specs, out_specs=out_specs, check_vma=False
    )
```

profile of v0, /device:TPU:0, one launch (start us, length us, event | category | flops | bytes accessed | tf_op | source)
XLA Modules:
  0.0 332.4 jit_solution(8118001672352756553)
XLA Ops:
  10.5 2.4 gather_fusion.1
  12.9 2.4 gather_fusion
  15.5 5.9 %collective-permute-start = (bf16[2,128,128]{2,1,0:T(8,128)(2,1)S(1)}, bf16[2,128,128]{2,1,0:T(8,128)(2,1)S(1)}, u32[]{:S(2)}, u32[]{:S(2)}) collective-permute-start(bf16[2,128,128]{2,1,0:T(8,128)(2,1)S(1)} %get-tuple-element.170), channel_id=1, source_target_pairs={{0,12},{4,16},{8,20},{12,24},{16,28},{1,13},{5,17},{9,21},{13,25},... | collective-permute-start | bytes 196616 | tf_op jit(solution)/shard_map/ppermute | solution.py:10
  22.8 3.5 %collective-permute-start.1 = (bf16[2,128,128]{2,1,0:T(8,128)(2,1)S(1)}, bf16[2,128,128]{2,1,0:T(8,128)(2,1)S(1)}, u32[]{:S(2)}, u32[]{:S(2)}) collective-permute-start(bf16[2,128,128]{2,1,0:T(8,128)(2,1)S(1)} %get-tuple-element.171), channel_id=1, source_target_pairs={{0,8},{4,12},{8,16},{12,20},{16,24},{20,28},{1,9},{5,13},{9,17},{1... | collective-permute-start | bytes 196616 | tf_op jit(solution)/shard_map/ppermute | solution.py:10
  26.2 4.4 %collective-permute-start.2 = (bf16[2,128,128]{2,1,0:T(8,128)(2,1)S(1)}, bf16[2,128,128]{2,1,0:T(8,128)(2,1)S(1)}, u32[]{:S(2)}, u32[]{:S(2)}) collective-permute-start(bf16[2,128,128]{2,1,0:T(8,128)(2,1)S(1)} %get-tuple-element.172), channel_id=1, source_target_pairs={{0,4},{4,8},{8,12},{12,16},{16,20},{20,24},{24,28},{1,5},{5,9},{9,... | collective-permute-start | bytes 196616 | tf_op jit(solution)/shard_map/ppermute | solution.py:10
  33.4 3.9 %collective-permute-done.3 = bf16[2,128,128]{2,1,0:T(8,128)(2,1)S(1)} collective-permute-done((bf16[2,128,128]{2,1,0:T(8,128)(2,1)S(1)}, bf16[2,128,128]{2,1,0:T(8,128)(2,1)S(1)}, u32[]{:S(2)}, u32[]{:S(2)}) %collective-permute-start.3) | collective-permute-done | bytes 65568 | tf_op jit(solution)/shard_map/ppermute | solution.py:10
  37.3 3.4 %collective-permute-done.4 = bf16[2,128,128]{2,1,0:T(8,128)(2,1)S(1)} collective-permute-done((bf16[2,128,128]{2,1,0:T(8,128)(2,1)S(1)}, bf16[2,128,128]{2,1,0:T(8,128)(2,1)S(1)}, u32[]{:S(2)}, u32[]{:S(2)}) %collective-permute-start.4) | collective-permute-done | bytes 65568 | tf_op jit(solution)/shard_map/ppermute | solution.py:10
  41.5 3.7 %fusion.44 = f32[4096,128]{0,1:T(8,128)S(1)} fusion(bf16[4096,512]{1,0:T(8,128)(2,1)} %param.15, bf16[512,128]{1,0:T(8,128)(2,1)S(1)} %copy-done.2), kind=kOutput, calls=%fused_computation.95 | convolution fusion | flops 536870912 | bytes 6422528 | tf_op jit(solution)/shard_map/dot_general | solution.py:90
  47.1 15.6 %all-gather.2.cloned.1.call-done = bf16[7,2,128,512]{3,2,1,0:T(8,128)(2,1)} async-done(((bf16[7,2,128,128]{3,2,1,0:T(8,128)(2,1)}), bf16[7,2,128,512]{3,2,1,0:T(8,128)(2,1)}) %all-gather.2.cloned.1.call-update) | async-done | bytes 1835024 | tf_op jit(solution)/shard_map/all_gather | solution.py:74
  66.9 181.4 %while.13 = (s32[]{:T(128)}, f32[4608,128]{1,0:T(8,128)S(1)}, f32[896,128]{1,0:T(8,128)S(1)}, s32[12]{0:T(128)S(1)}, s32[6144]{0:T(1024)}, /*index=5*/s32[6144]{...) while((s32[]{:T(128)}, f32[4608,128]{1,0:T(8,128)S(1)}, ...), condition=%wide.region_1.2_spmd.clone, body=%wide.region_0.1_spmd.clone.sunk | while | flops 858358272 | bytes 7361323 | solution.py:132
  75.3 1.9 fusion.74
  90.4 1.9 fusion.74
  105.5 1.9 fusion.74
  120.7 1.9 fusion.74
  135.8 1.9 fusion.74
  151.0 1.9 fusion.74
  166.1 1.9 fusion.74
  181.2 1.9 fusion.74
  196.4 1.9 fusion.74
  211.5 1.9 fusion.74
  226.7 1.9 fusion.74
  241.8 1.9 fusion.74
  249.0 1.9 convolution_convert_fusion.1
  252.3 4.1 %convolution_convert_fusion = bf16[4096,512]{1,0:T(8,128)(2,1)} fusion(bf16[512,128]{1,0:T(8,128)(2,1)} %param.23, f32[4608,128]{1,0:T(8,128)S(1)} %get-tuple-element.70), kind=kOutput, calls=%fused_computation.29 | convolution fusion | flops 538968064 | bytes 5373952 | tf_op jit(solution)/shard_map/dot_general | solution.py:154
  256.5 6.5 %copy.39 = bf16[4096,512]{0,1:T(8,128)(2,1)} copy(bf16[4096,512]{1,0:T(8,128)(2,1)} %convolution_convert_fusion) | data formatting | bytes 8388608
  263.0 13.5 %reduce-scatter.9.cloned.1.call-done = bf16[128,896]{1,0:T(8,128)(2,1)} async-done(((bf16[512,896]{1,0:T(8,128)(2,1)}), bf16[128,896]{1,0:T(8,128)(2,1)}) %reduce-scatter.9.cloned.1.call-update) | async-done | bytes 229392
  282.1 4.5 %collective-permute-start.9 = (bf16[128,128]{1,0:T(8,128)(2,1)S(1)}, bf16[128,128]{1,0:T(8,128)(2,1)S(1)}, u32[]{:S(2)}, u32[]{:S(2)}) collective-permute-start(bf16[128,128]{1,0:T(8,128)(2,1)S(1)} %copy.55), channel_id=1, source_target_pairs={{0,4},{4,8},{8,12},{12,16},{16,20},{20,24},{24,28},{1,5},{5,9},{9,... | collective-permute-start | bytes 98312 | tf_op jit(solution)/shard_map/ppermute | solution.py:10
  286.6 4.6 %collective-permute-start.10 = (bf16[128,128]{1,0:T(8,128)(2,1)S(1)}, bf16[128,128]{1,0:T(8,128)(2,1)S(1)}, u32[]{:S(2)}, u32[]{:S(2)}) collective-permute-start(bf16[128,128]{1,0:T(8,128)(2,1)S(1)} %copy.56), channel_id=1, source_target_pairs={{0,8},{4,12},{8,16},{12,20},{16,24},{20,28},{1,9},{5,13},{9,17},{1... | collective-permute-start | bytes 98312 | tf_op jit(solution)/shard_map/ppermute | solution.py:10
  291.3 6.5 %collective-permute-start.11 = (bf16[128,128]{1,0:T(8,128)(2,1)S(1)}, bf16[128,128]{1,0:T(8,128)(2,1)S(1)}, u32[]{:S(2)}, u32[]{:S(2)}) collective-permute-start(bf16[128,128]{1,0:T(8,128)(2,1)S(1)} %copy.57), channel_id=1, source_target_pairs={{0,12},{4,16},{8,20},{12,24},{16,28},{1,13},{5,17},{9,21},{13,25},... | collective-permute-start | bytes 98312 | tf_op jit(solution)/shard_map/ppermute | solution.py:10
  299.1 7.6 %scatter_custom_fusion = f32[640,128]{1,0:T(8,128)S(1)} fusion(s32[896]{0:T(1024)S(1)} %bitcast.102, bf16[896,128]{1,0:T(8,128)(2,1)S(1)} %bitcast.99, f32[]{:T(128)} %constant.6.clone.1, pred[896]{0:T(1024)(128)(4,1)S(1)} %bitcast.103), kind=kCustom, calls=%fused_computation.52 | custom fusion | flops 344064 | bytes 559104 | tf_op jit(solution)/shard_map/scatter-add | solution.py:151
  307.4 16.2 %reduce-scatter.7.cloned.1.call-done = bf16[128,4096]{1,0:T(8,128)(2,1)} async-done(((bf16[512,4096]{1,0:T(8,128)(2,1)}), bf16[128,4096]{1,0:T(8,128)(2,1)}) %reduce-scatter.7.cloned.1.call-update) | async-done | bytes 1048592
  323.6 2.3 copy.40
  (203 shorter events, 148.1 us)
Async XLA Ops:
  7.2 5.7 %copy-start = (bf16[640,128]{1,0:T(8,128)(2,1)S(1)}, bf16[640,128]{1,0:T(8,128)(2,1)}, u32[]{:S(2)}) copy-start(bf16[640,128]{1,0:T(8,128)(2,1)} %param.17) | copy-start | bytes 491524
  7.2 55.5 %all-gather.2.cloned.1.call-start = ((), (), s32[]{:S(2)}) async-start(), calls=%async_computation.2 | async-start | bytes 2293760 | tf_op jit(solution)/shard_map/all_gather | solution.py:74
  12.9 28.7 %copy-start.2 = (bf16[512,128]{1,0:T(8,128)(2,1)S(1)}, bf16[512,128]{1,0:T(8,128)(2,1)}, u32[]{:S(2)}) copy-start(bf16[512,128]{1,0:T(8,128)(2,1)} %param.23) | copy-start | bytes 393220
  15.5 16.5 %collective-permute-start = (bf16[2,128,128]{2,1,0:T(8,128)(2,1)S(1)}, bf16[2,128,128]{2,1,0:T(8,128)(2,1)S(1)}, u32[]{:S(2)}, u32[]{:S(2)}) collective-permute-start(bf16[2,128,128]{2,1,0:T(8,128)(2,1)S(1)} %get-tuple-element.170), channel_id=1, source_target_pairs={{0,12},{4,16},{8,20},{12,24},{16,28},{1,13},{5,17},{9,21},{13,25},... | collective-permute-start | bytes 196616 | tf_op jit(solution)/shard_map/ppermute | solution.py:10
  21.5 19.2 %collective-permute-start.5 = (bf16[2,128,128]{2,1,0:T(8,128)(2,1)S(1)}, bf16[2,128,128]{2,1,0:T(8,128)(2,1)S(1)}, u32[]{:S(2)}, u32[]{:S(2)}) collective-permute-start(bf16[2,128,128]{2,1,0:T(8,128)(2,1)S(1)} %get-tuple-element.169), channel_id=1, source_target_pairs={{12,0},{16,4},{20,8},{24,12},{28,16},{13,1},{17,5},{21,9},{25,13},... | collective-permute-start | bytes 196616 | tf_op jit(solution)/shard_map/ppermute | solution.py:10
  22.8 10.6 %collective-permute-start.1 = (bf16[2,128,128]{2,1,0:T(8,128)(2,1)S(1)}, bf16[2,128,128]{2,1,0:T(8,128)(2,1)S(1)}, u32[]{:S(2)}, u32[]{:S(2)}) collective-permute-start(bf16[2,128,128]{2,1,0:T(8,128)(2,1)S(1)} %get-tuple-element.171), channel_id=1, source_target_pairs={{0,8},{4,12},{8,16},{12,20},{16,24},{20,28},{1,9},{5,13},{9,17},{1... | collective-permute-start | bytes 196616 | tf_op jit(solution)/shard_map/ppermute | solution.py:10
  26.2 7.1 %collective-permute-start.2 = (bf16[2,128,128]{2,1,0:T(8,128)(2,1)S(1)}, bf16[2,128,128]{2,1,0:T(8,128)(2,1)S(1)}, u32[]{:S(2)}, u32[]{:S(2)}) collective-permute-start(bf16[2,128,128]{2,1,0:T(8,128)(2,1)S(1)} %get-tuple-element.172), channel_id=1, source_target_pairs={{0,4},{4,8},{8,12},{12,16},{16,20},{20,24},{24,28},{1,5},{5,9},{9,... | collective-permute-start | bytes 196616 | tf_op jit(solution)/shard_map/ppermute | solution.py:10
  30.7 6.6 %collective-permute-start.3 = (bf16[2,128,128]{2,1,0:T(8,128)(2,1)S(1)}, bf16[2,128,128]{2,1,0:T(8,128)(2,1)S(1)}, u32[]{:S(2)}, u32[]{:S(2)}) collective-permute-start(bf16[2,128,128]{2,1,0:T(8,128)(2,1)S(1)} %get-tuple-element.173), channel_id=1, source_target_pairs={{4,0},{8,4},{12,8},{16,12},{20,16},{24,20},{28,24},{5,1},{9,5},{13... | collective-permute-start | bytes 196616 | tf_op jit(solution)/shard_map/ppermute | solution.py:10
  32.0 8.6 %collective-permute-start.4 = (bf16[2,128,128]{2,1,0:T(8,128)(2,1)S(1)}, bf16[2,128,128]{2,1,0:T(8,128)(2,1)S(1)}, u32[]{:S(2)}, u32[]{:S(2)}) collective-permute-start(bf16[2,128,128]{2,1,0:T(8,128)(2,1)S(1)} %get-tuple-element.174), channel_id=1, source_target_pairs={{8,0},{12,4},{16,8},{20,12},{24,16},{28,20},{9,1},{13,5},{17,9},{2... | collective-permute-start | bytes 196616 | tf_op jit(solution)/shard_map/ppermute | solution.py:10
  40.7 0.8 copy-start.1
  41.5 235.0 %reduce-scatter.9.cloned.1.call-start = ((), (), s32[]{:S(2)}) async-start(), calls=%async_computation.4 | async-start | bytes 1146880
  47.1 17.2 %copy-start.3 = (bf16[512,128]{1,0:T(8,128)(2,1)S(1)}, bf16[512,128]{1,0:T(8,128)(2,1)}, u32[]{:S(2)}) copy-start(bf16[512,128]{1,0:T(8,128)(2,1)} %param.24) | copy-start | bytes 393220
  47.1 17.6 %copy-start.5 = (bf16[128,512]{1,0:T(8,128)(2,1)S(1)}, bf16[128,512]{1,0:T(8,128)(2,1)}, u32[]{:S(2)}) copy-start(bf16[128,512]{1,0:T(8,128)(2,1)} %param.27) | copy-start | bytes 393220
  65.4 1.5 copy-start.6
  65.4 1.5 copy-start.7
  248.3 0.8 copy-start.4
  252.3 71.3 %reduce-scatter.7.cloned.1.call-start = ((), (), s32[]{:S(2)}) async-start(), calls=%async_computation.3 | async-start | bytes 5242880
  277.4 13.8 %collective-permute-start.6 = (bf16[128,128]{1,0:T(8,128)(2,1)S(1)}, bf16[128,128]{1,0:T(8,128)(2,1)S(1)}, u32[]{:S(2)}, u32[]{:S(2)}) collective-permute-start(bf16[128,128]{1,0:T(8,128)(2,1)S(1)} %copy.51), channel_id=1, source_target_pairs={{12,0},{16,4},{20,8},{24,12},{28,16},{13,1},{17,5},{21,9},{25,13},... | collective-permute-start | bytes 98312 | tf_op jit(solution)/shard_map/ppermute | solution.py:10
  279.5 18.3 %collective-permute-start.7 = (bf16[128,128]{1,0:T(8,128)(2,1)S(1)}, bf16[128,128]{1,0:T(8,128)(2,1)S(1)}, u32[]{:S(2)}, u32[]{:S(2)}) collective-permute-start(bf16[128,128]{1,0:T(8,128)(2,1)S(1)} %copy.52), channel_id=1, source_target_pairs={{8,0},{12,4},{16,8},{20,12},{24,16},{28,20},{9,1},{13,5},{17,9},{2... | collective-permute-start | bytes 98312 | tf_op jit(solution)/shard_map/ppermute | solution.py:10
  280.8 17.0 %collective-permute-start.8 = (bf16[128,128]{1,0:T(8,128)(2,1)S(1)}, bf16[128,128]{1,0:T(8,128)(2,1)S(1)}, u32[]{:S(2)}, u32[]{:S(2)}) collective-permute-start(bf16[128,128]{1,0:T(8,128)(2,1)S(1)} %copy.53), channel_id=1, source_target_pairs={{4,0},{8,4},{12,8},{16,12},{20,16},{24,20},{28,24},{5,1},{9,5},{13... | collective-permute-start | bytes 98312 | tf_op jit(solution)/shard_map/ppermute | solution.py:10
  282.1 15.7 %collective-permute-start.9 = (bf16[128,128]{1,0:T(8,128)(2,1)S(1)}, bf16[128,128]{1,0:T(8,128)(2,1)S(1)}, u32[]{:S(2)}, u32[]{:S(2)}) collective-permute-start(bf16[128,128]{1,0:T(8,128)(2,1)S(1)} %copy.55), channel_id=1, source_target_pairs={{0,4},{4,8},{8,12},{12,16},{16,20},{20,24},{24,28},{1,5},{5,9},{9,... | collective-permute-start | bytes 98312 | tf_op jit(solution)/shard_map/ppermute | solution.py:10
  286.6 11.2 %collective-permute-start.10 = (bf16[128,128]{1,0:T(8,128)(2,1)S(1)}, bf16[128,128]{1,0:T(8,128)(2,1)S(1)}, u32[]{:S(2)}, u32[]{:S(2)}) collective-permute-start(bf16[128,128]{1,0:T(8,128)(2,1)S(1)} %copy.56), channel_id=1, source_target_pairs={{0,8},{4,12},{8,16},{12,20},{16,24},{20,28},{1,9},{5,13},{9,17},{1... | collective-permute-start | bytes 98312 | tf_op jit(solution)/shard_map/ppermute | solution.py:10
  291.3 7.9 %collective-permute-start.11 = (bf16[128,128]{1,0:T(8,128)(2,1)S(1)}, bf16[128,128]{1,0:T(8,128)(2,1)S(1)}, u32[]{:S(2)}, u32[]{:S(2)}) collective-permute-start(bf16[128,128]{1,0:T(8,128)(2,1)S(1)} %copy.57), channel_id=1, source_target_pairs={{0,12},{4,16},{8,20},{12,24},{16,28},{1,13},{5,17},{9,21},{13,25},... | collective-permute-start | bytes 98312 | tf_op jit(solution)/shard_map/ppermute | solution.py:10
Sparse Core Ops, SparseCore 0:
  41.6 21.0 all-gather.1
  252.4 24.0 reduce-scatter.8
  279.0 44.5 reduce-scatter.6
where the time goes:
time: 336 us; the launch traced here: 332 us
  matrix products  84.5 us (25%)
  local copies, waits for them, and re-layouts  77.5 us (23%)
  waiting for transfers between devices  53.8 us (16%)
  starting transfers between devices  37.3 us (11%)
  loops' own time  34 us (10%)
  other arithmetic  31.1 us (9%)
  between operations  14.2 us (4%)
    ppermute x12, starting transfers between devices, shifted(): return lax.ppermute(shard, axis, pairs)  37.2 us
    another operation x1, loops' own time, per_device(): lax.scan(one_block, initial, jnp.arange(block_count, dtype=jnp.int32))  34 us
    unnamed x5, waiting for transfers between devices  29.7 us
    dot_general x12, matrix products, one_block(): jnp.dot(slot_pick, slot_split, preferred_element_type=jnp.float32)  23.2 us
    dynamic_update_slice x12, local copies, waits for them, and re-layouts, one_block(): lax.dynamic_update_slice_in_dim(sender_acc, current + sender_part, anchor...  22.7 us
    sub x12, other arithmetic, one_block(): senders - anchor  17.4 us
    dot_general x12, matrix products, one_block(): jnp.dot(edge_rows, w_edge, preferred_element_type=jnp.float32)  16.6 us
    dot_general x12, matrix products, one_block(): grid_both = jnp.dot(grid_pick, window, preferred_element_type=jnp.float32)  16.6 us
  transfers between devices with their start and end apart: 15, of which 6 were waited for; matrix products, arithmetic and copies ran while one was open for 8% of the time, Pallas kernels for 0%

commit v1 on v0

v1 whole, which is shorter than its diff:
```python
import functools
import math

import jax
import jax.numpy as jnp
from jax import lax
from jax.experimental import pallas as pl
from jax.experimental.pallas import tpu as pltpu
from jax.sharding import PartitionSpec as P


def shifted(shard, axis, by):
    devices = lax.axis_size(axis)
    pairs = [(i, i + by) for i in range(devices) if 0 <= i + by < devices]
    return lax.ppermute(shard, axis, pairs)


def silu_slope(pre_act):
    sigmoid_value = jax.nn.sigmoid(pre_act)
    return sigmoid_value * (1.0 + pre_act * (1.0 - sigmoid_value))


def per_offset(blocks, reach, sign, mover):
    results = []
    for offset in range(blocks.shape[0]):
        amount = sign * (reach - offset)
        if amount == 0:
            results.append(blocks[offset])
        else:
            results.append(mover(blocks[offset], amount))
    return jnp.stack(results)


def largest_divisor(total, highest):
    width = highest
    while total % width:
        width //= 2
    return width


def edge_kernel(
    anchors,
    sender_ref,
    slot_ref,
    grid_ref,
    edge_ref,
    table_ref,
    w_send_ref,
    w_edge_ref,
    bias_ref,
    sender_out,
    slot_out,
    proj,
    sender_acc,
    slot_acc,
    *,
    grid_blocks,
    grid_rows,
    block_count,
):
    step = pl.program_id(0)
    width = edge_ref.shape[0]
    hidden = w_send_ref.shape[1]
    slot_count = table_ref.shape[0]

    @pl.when(step == 0)
    def _():
        proj[pl.ds(grid_rows, width), :] = jnp.zeros((width, hidden), jnp.float32)
        sender_acc[...] = jnp.zeros_like(sender_acc)
        slot_acc[...] = jnp.zeros_like(slot_acc)

    @pl.when(step < grid_blocks)
    def _():
        proj[pl.ds(pl.multiple_of(step * width, width), width), :] = jnp.dot(
            grid_ref[...], w_send_ref[...], preferred_element_type=jnp.float32
        )

    anchor = anchors[step]
    local = sender_ref[0].astype(jnp.float32) - anchor.astype(jnp.float32)
    slots = slot_ref[0].astype(jnp.float32)
    lanes = lax.broadcasted_iota(jnp.int32, (width, 128), 1).astype(jnp.float32)
    local_col = jnp.broadcast_to(local, (128, width)).T
    slots_col = jnp.broadcast_to(slots, (128, width)).T

    def rows_pick(column, count):
        parts = [
            jnp.where(column - 128.0 * j == lanes, 1.0, 0.0).astype(jnp.bfloat16)
            for j in range(count // 128)
        ]
        return jnp.concatenate(parts, axis=1)

    def cols_pick(row, count):
        rows = lax.broadcasted_iota(jnp.int32, (count, width), 0).astype(jnp.float32)
        return jnp.where(rows == row, 1.0, 0.0).astype(jnp.bfloat16)

    window = proj[pl.ds(anchor, width), :].astype(jnp.bfloat16)
    pre_act = jnp.dot(edge_ref[...], w_edge_ref[...], preferred_element_type=jnp.float32)
    pre_act += jnp.dot(rows_pick(local_col, width), window, preferred_element_type=jnp.float32)
    both = jnp.dot(
        rows_pick(slots_col, slot_count), table_ref[...], preferred_element_type=jnp.float32
    )
    pre_act += both[:, :hidden] + bias_ref[...]
    edge_grad = (both[:, hidden:] * silu_slope(pre_act)).astype(jnp.bfloat16)
    sender_acc[pl.ds(anchor, width), :] += jnp.dot(
        cols_pick(local, width), edge_grad, preferred_element_type=jnp.float32
    )
    slot_acc[...] += jnp.dot(
        cols_pick(slots, slot_count), edge_grad, preferred_element_type=jnp.float32
    )

    @pl.when(step == block_count - 1)
    def _():
        sender_out[...] = sender_acc[pl.ds(0, grid_rows), :].astype(sender_out.dtype)
        slot_out[...] = slot_acc[...].astype(slot_out.dtype)


def edge_pass(grid_latent, edge_latent, table, edge_sender, edge_slot, w_send, w_edge, bias, slot_type):
    grid_rows, latent = grid_latent.shape
    edge_count = edge_latent.shape[0]
    hidden = w_send.shape[1]
    slot_count = table.shape[0]
    width = largest_divisor(math.gcd(edge_count, grid_rows), 512)
    block_count = edge_count // width
    grid_blocks = grid_rows // width
    senders = edge_sender.reshape(block_count, 1, width)
    slots = edge_slot.reshape(block_count, 1, width)
    return pl.pallas_call(
        functools.partial(
            edge_kernel, grid_blocks=grid_blocks, grid_rows=grid_rows, block_count=block_count
        ),
        grid_spec=pltpu.PrefetchScalarGridSpec(
            num_scalar_prefetch=1,
            grid=(block_count,),
            in_specs=[
                pl.BlockSpec((1, 1, width), lambda i, a: (i, 0, 0)),
                pl.BlockSpec((1, 1, width), lambda i, a: (i, 0, 0)),
                pl.BlockSpec((width, latent), lambda i, a: (jnp.minimum(i, grid_blocks - 1), 0)),
                pl.BlockSpec((width, latent), lambda i, a: (i, 0)),
                pl.BlockSpec(table.shape, lambda i, a: (0, 0)),
                pl.BlockSpec(w_send.shape, lambda i, a: (0, 0)),
                pl.BlockSpec(w_edge.shape, lambda i, a: (0, 0)),
                pl.BlockSpec((1, hidden), lambda i, a: (0, 0)),
            ],
            out_specs=[
                pl.BlockSpec((grid_rows, hidden), lambda i, a: (0, 0)),
                pl.BlockSpec((slot_count, hidden), lambda i, a: (0, 0)),
            ],
            scratch_shapes=[
                pltpu.VMEM((grid_rows + width, hidden), jnp.float32),
                pltpu.VMEM((grid_rows + width, hidden), jnp.float32),
                pltpu.VMEM((slot_count, hidden), jnp.float32),
            ],
        ),
        out_shape=[
            jax.ShapeDtypeStruct((grid_rows, hidden), jnp.bfloat16),
            jax.ShapeDtypeStruct((slot_count, hidden), slot_type),
        ],
        compiler_params=pltpu.CompilerParams(dimension_semantics=("arbitrary",)),
        cost_estimate=pl.CostEstimate(
            flops=10_000_000_000, bytes_accessed=12_000_000, transcendentals=0
        ),
        name="edge_pass",
    )(senders[:, 0, 0], senders, slots, grid_latent, edge_latent, table, w_send, w_edge, bias.reshape(1, hidden))


def per_device(
    grid_latent,
    edge_latent,
    mesh_latent,
    mesh_grad,
    counts,
    request,
    edge_sender,
    edge_slot,
    w_send,
    w_recv,
    w_edge,
    edge_bias,
    w_out,
):
    span = request.shape[1]
    capacity = request.shape[2]
    reach = (span - 1) // 2
    node_count = mesh_latent.shape[0]
    latent = grid_latent.shape[1]
    slot_count = span * capacity
    scaled_grad = (mesh_grad.astype(jnp.float32) / counts.astype(jnp.float32)[:, None]).astype(
        jnp.bfloat16
    )
    wanted = request[0]
    live_slot = (wanted >= 0)[:, :, None]
    picker = jnp.maximum(wanted, 0)
    flat_live = live_slot.reshape(slot_count, 1)
    flat_picker = picker.reshape(-1)
    send_both = jnp.stack(
        [
            jnp.where(live_slot, mesh_latent[picker], 0),
            jnp.where(live_slot, scaled_grad[picker], 0),
        ],
        axis=1,
    )
    got_part = per_offset(send_both, reach, 1, lambda block, amount: shifted(block, "band", amount))
    got = lax.all_gather(got_part, "mp", axis=3, tiled=True)
    slot_proj = jnp.dot(
        got[:, 0].reshape(slot_count, latent), w_recv, preferred_element_type=jnp.float32
    )
    slot_back = jnp.dot(
        got[:, 1].reshape(slot_count, latent), w_out.T, preferred_element_type=jnp.float32
    )
    table = jnp.concatenate([slot_proj, slot_back], axis=1).astype(jnp.bfloat16)
    sender_sum, slot_sum = edge_pass(
        grid_latent, edge_latent, table, edge_sender, edge_slot, w_send, w_edge, edge_bias, jnp.float32
    )
    recv_wide = w_recv.astype(jnp.float32)
    slot_term = jnp.dot(slot_sum, recv_wide.T, precision=lax.Precision.HIGHEST)
    slot_share = lax.psum_scatter(
        slot_term.astype(jnp.bfloat16), "mp", scatter_dimension=1, tiled=True
    ).astype(jnp.float32)
    part_cols = slot_share.shape[1]
    returned = per_offset(
        slot_share.reshape(span, capacity, part_cols),
        reach,
        -1,
        lambda block, amount: shifted(block.astype(jnp.bfloat16), "band", amount).astype(
            block.dtype
        ),
    )
    kept_rows = jnp.where(flat_live, returned.reshape(slot_count, part_cols), 0.0)
    node_grad = jax.ops.segment_sum(kept_rows, flat_picker, num_segments=node_count).astype(
        jnp.bfloat16
    )
    grid_term = jnp.dot(sender_sum, w_send.T, preferred_element_type=jnp.float32)
    grid_grad = lax.psum_scatter(
        grid_term.astype(jnp.bfloat16), "mp", scatter_dimension=1, tiled=True
    )
    return (grid_grad, node_grad)


def solution(mesh):
    in_specs = (
        P("band", None),
        P("band", None),
        P("band", "mp"),
        P("band", "mp"),
        P("band"),
        P("band", None, None),
        P("band"),
        P("band"),
        P(None, "mp"),
        P(None, "mp"),
        P(None, "mp"),
        P("mp"),
        P("mp", None),
    )
    out_specs = (P("band", "mp"), P("band", "mp"))
    return jax.shard_map(
        per_device, mesh=mesh, in_specs=in_specs, out_specs=out_specs, check_vma=False
    )
```

time: 336 us -> 172 us (0.51)
  matrix products: 84.5 us -> 6.01 us
  local copies, waits for them, and re-layouts: 77.5 us -> 20.6 us
  loops' own time: 34 us -> 0 us
  Pallas kernels: 0 us -> 22 us
  other arithmetic: 31.1 us -> 12.5 us
  waiting for transfers between devices: 53.8 us -> 58.9 us
    dot_general x61 -> x0, matrix products: 77.5 us -> none  [the longest x12 23.2 us: one_block(): jnp.dot(slot_pick, slot_split, preferred_element_type=jnp.float32)]
    another operation x1 -> x0, loops' own time: 34 us -> none  [per_device(): lax.scan(one_block, initial, jnp.arange(block_count, dtype=jnp.int32))]
    dynamic_slice x36 -> x0, local copies, waits for them, and re-layouts: 26.3 us -> none  [the longest x12 9.17 us: one_block(): slot_ids = lax.dynamic_slice_in_dim(slot_pad, first_row, width_rows, 0)]
    dynamic_update_slice x12 -> x0, local copies, waits for them, and re-layouts: 22.7 us -> none  [one_block(): lax.dynamic_update_slice_in_dim(sender_acc, current + sender_part, anchor...]
    pallas_call x0 -> x1, Pallas kernels: none -> 22 us  [edge_pass(): pl.pallas_call(functools.partial(edge_kernel, grid_blocks=grid_blocks, gr...]
    sub x12 -> x0, other arithmetic: 17.4 us -> none  [one_block(): senders - anchor]
    slice x12 -> x1, local copies, waits for them, and re-layouts: 7.12 us -> 1.52 us  [edge_pass(): senders[:, 0, 0]]
    all_gather x1, waiting for transfers between devices: 15.6 us -> 19.6 us  [per_device(): got = lax.all_gather(got_part, 'mp', axis=3, tiled=True)]
  transfers between devices with their start and end apart: 15 -> 15, of which waited for: 6 -> 6; matrix products, arithmetic and copies ran while one was open for 8% -> 12% of each run, Pallas kernels for 0% -> 0%
where the time goes in v1:
time: 172 us; the launch traced here: 171 us
  waiting for transfers between devices  58.9 us (34%)
  starting transfers between devices  37.2 us (22%)
  Pallas kernels  22 us (13%)
  local copies, waits for them, and re-layouts  20.6 us (12%)
  between operations  14.2 us (8%)
  other arithmetic  12.5 us (7%)
  matrix products  6.01 us (3%)
    ppermute x12, starting transfers between devices, shifted(): return lax.ppermute(shard, axis, pairs)  37 us
    unnamed x5, waiting for transfers between devices  30.6 us
    pallas_call x1, Pallas kernels, edge_pass(): pl.pallas_call(functools.partial(edge_kernel, grid_blocks=grid_blocks, gr...  22 us
    all_gather x1, waiting for transfers between devices, per_device(): got = lax.all_gather(got_part, 'mp', axis=3, tiled=True)  19.6 us
    unnamed x34, local copies, waits for them, and re-layouts  11.8 us
    ppermute x12, waiting for transfers between devices, shifted(): return lax.ppermute(shard, axis, pairs)  8.71 us
    scatter-add x1, other arithmetic, per_device(): jax.ops.segment_sum(kept_rows, flat_picker, num_segments=node_count)  7.59 us
  transfers between devices with their start and end apart: 15, of which 6 were waited for; matrix products, arithmetic and copies ran while one was open for 12% of the time, Pallas kernels for 0%

profile of v1, /device:TPU:0, one launch (start us, length us, event | category | flops | bytes accessed | tf_op | source)
XLA Modules:
  0.0 171.3 jit_solution(9053837254513496287)
XLA Ops:
  9.4 1.1 divide_convert_fusion
  10.5 2.4 %gather_fusion.1 = bf16[896,128]{1,0:T(8,128)(2,1)S(1)} fusion(bf16[640,128]{1,0:T(8,128)(2,1)S(1)} %divide_convert_fusion, s32[1024]{0:T(1024)S(1)} %pad_clamp_fusion), kind=kCustom, calls=%fused_computation.1 | custom fusion | bytes 462336 | tf_op jit(solution)/shard_map/gather | solution.py:198
  12.9 2.4 %gather_fusion = bf16[896,128]{1,0:T(8,128)(2,1)S(1)} fusion(bf16[640,128]{1,0:T(8,128)(2,1)S(1)} %copy-done, s32[1024]{0:T(1024)S(1)} %pad_clamp_fusion), kind=kCustom, calls=%fused_computation | custom fusion | bytes 462336 | tf_op jit(solution)/shard_map/gather | solution.py:197
  15.5 5.9 %collective-permute-start = (bf16[2,128,128]{2,1,0:T(8,128)(2,1)S(1)}, bf16[2,128,128]{2,1,0:T(8,128)(2,1)S(1)}, u32[]{:S(2)}, u32[]{:S(2)}) collective-permute-start(bf16[2,128,128]{2,1,0:T(8,128)(2,1)S(1)} %get-tuple-element.9), channel_id=1, source_target_pairs={{0,12},{4,16},{8,20},{12,24},{16,28},{1,13},{5,17},{9,21},{13,25},... | collective-permute-start | bytes 196616 | tf_op jit(solution)/shard_map/ppermute | solution.py:15
  21.5 1.3 collective-permute-start.5
  22.8 3.5 %collective-permute-start.1 = (bf16[2,128,128]{2,1,0:T(8,128)(2,1)S(1)}, bf16[2,128,128]{2,1,0:T(8,128)(2,1)S(1)}, u32[]{:S(2)}, u32[]{:S(2)}) collective-permute-start(bf16[2,128,128]{2,1,0:T(8,128)(2,1)S(1)} %get-tuple-element.10), channel_id=1, source_target_pairs={{0,8},{4,12},{8,16},{12,20},{16,24},{20,28},{1,9},{5,13},{9,17},{1... | collective-permute-start | bytes 196616 | tf_op jit(solution)/shard_map/ppermute | solution.py:15
  26.3 4.4 %collective-permute-start.2 = (bf16[2,128,128]{2,1,0:T(8,128)(2,1)S(1)}, bf16[2,128,128]{2,1,0:T(8,128)(2,1)S(1)}, u32[]{:S(2)}, u32[]{:S(2)}) collective-permute-start(bf16[2,128,128]{2,1,0:T(8,128)(2,1)S(1)} %get-tuple-element.11), channel_id=1, source_target_pairs={{0,4},{4,8},{8,12},{12,16},{16,20},{20,24},{24,28},{1,5},{5,9},{9,... | collective-permute-start | bytes 196616 | tf_op jit(solution)/shard_map/ppermute | solution.py:15
  30.7 1.3 collective-permute-start.3
  32.0 1.3 collective-permute-start.4
  33.4 3.9 %collective-permute-done.3 = bf16[2,128,128]{2,1,0:T(8,128)(2,1)S(1)} collective-permute-done((bf16[2,128,128]{2,1,0:T(8,128)(2,1)S(1)}, bf16[2,128,128]{2,1,0:T(8,128)(2,1)S(1)}, u32[]{:S(2)}, u32[]{:S(2)}) %collective-permute-start.3) | collective-permute-done | bytes 65568 | tf_op jit(solution)/shard_map/ppermute | solution.py:15
  37.3 3.4 %collective-permute-done.4 = bf16[2,128,128]{2,1,0:T(8,128)(2,1)S(1)} collective-permute-done((bf16[2,128,128]{2,1,0:T(8,128)(2,1)S(1)}, bf16[2,128,128]{2,1,0:T(8,128)(2,1)S(1)}, u32[]{:S(2)}, u32[]{:S(2)}) %collective-permute-start.4) | collective-permute-done | bytes 65568 | tf_op jit(solution)/shard_map/ppermute | solution.py:15
  41.5 1.5 slice_reduce_fusion.anchors
  43.1 19.6 %all-gather.2.cloned.1.call-done = bf16[7,2,128,512]{3,2,1,0:T(8,128)(2,1)} async-done(((bf16[7,2,128,128]{3,2,1,0:T(8,128)(2,1)}), bf16[7,2,128,512]{3,2,1,0:T(8,128)(2,1)}) %all-gather.2.cloned.1.call-update) | async-done | bytes 1835024 | tf_op jit(solution)/shard_map/all_gather | solution.py:203
  62.7 1.6 fusion.17
  65.1 0.8 pad_maximum_fusion.table_ref
  65.9 22.0 %edge_pass.1 = (bf16[4096,128]{1,0:T(8,128)(2,1)}, f32[896,128]{1,0:T(8,128)}) custom-call(s32[12]{0:T(128)} %slice_reduce_fusion.anchors, s32[12,1,512]{2,1,0:T(1,128)} %bitcast.90, s32[12,1,512]{2,1,0:T(1,128)} %bitcast.91, bf16[4096,512]{1,0:T(8,128)(2,1)} %grid_ref.1, bf16[6144,512]{1,0:T(8,128)(2,1)} %edge_ref.1, ...), custom_call_target="tpu_custom_call" | custom-call | flops 10000000000 | bytes 12000000 | tf_op jit(solution)/shard_map/edge_pass/pallas_call | solution.py:127
  87.9 2.0 %convolution_convert_fusion.1 = bf16[896,512]{1,0:T(8,128)(2,1)S(1)} fusion(f32[896,128]{1,0:T(8,128)} %get-tuple-element.5, bf16[512,128]{1,0:T(8,128)(2,1)S(1)} %copy-done.3), kind=kOutput, calls=%fused_computation.4 | convolution fusion | flops 705101824 | bytes 1507328 | tf_op jit(solution)/shard_map/dot_general | solution.py:215
  89.9 1.3 copy.43
  91.3 3.2 %convolution_convert_fusion = bf16[4096,512]{1,0:T(8,128)(2,1)} fusion(bf16[4096,128]{1,0:T(8,128)(2,1)S(1)} %copy-done.1, bf16[512,128]{1,0:T(8,128)(2,1)S(1)} %copy-done.4), kind=kOutput, calls=%fused_computation.3 | convolution fusion | flops 538968064 | bytes 5373952 | tf_op jit(solution)/shard_map/dot_general | solution.py:232
  94.5 6.5 %copy.41 = bf16[4096,512]{0,1:T(8,128)(2,1)} copy(bf16[4096,512]{1,0:T(8,128)(2,1)} %convolution_convert_fusion) | data formatting | bytes 8388608
  101.0 14.4 %reduce-scatter.9.cloned.1.call-done = bf16[128,896]{1,0:T(8,128)(2,1)} async-done(((bf16[512,896]{1,0:T(8,128)(2,1)}), bf16[128,896]{1,0:T(8,128)(2,1)}) %reduce-scatter.9.cloned.1.call-update) | async-done | bytes 229392
  115.4 0.9 fusion.18
  116.4 1.3 collective-permute-start.6
  118.4 1.3 collective-permute-start.7
  119.7 1.3 collective-permute-start.8
  121.0 4.5 %collective-permute-start.9 = (bf16[128,128]{1,0:T(8,128)(2,1)S(1)}, bf16[128,128]{1,0:T(8,128)(2,1)S(1)}, u32[]{:S(2)}, u32[]{:S(2)}) collective-permute-start(bf16[128,128]{1,0:T(8,128)(2,1)S(1)} %copy.56), channel_id=1, source_target_pairs={{0,4},{4,8},{8,12},{12,16},{16,20},{20,24},{24,28},{1,5},{5,9},{9,... | collective-permute-start | bytes 98312 | tf_op jit(solution)/shard_map/ppermute | solution.py:15
  125.6 4.6 %collective-permute-start.10 = (bf16[128,128]{1,0:T(8,128)(2,1)S(1)}, bf16[128,128]{1,0:T(8,128)(2,1)S(1)}, u32[]{:S(2)}, u32[]{:S(2)}) collective-permute-start(bf16[128,128]{1,0:T(8,128)(2,1)S(1)} %copy.57), channel_id=1, source_target_pairs={{0,8},{4,12},{8,16},{12,20},{16,24},{20,28},{1,9},{5,13},{9,17},{1... | collective-permute-start | bytes 98312 | tf_op jit(solution)/shard_map/ppermute | solution.py:15
  130.2 6.3 %collective-permute-start.11 = (bf16[128,128]{1,0:T(8,128)(2,1)S(1)}, bf16[128,128]{1,0:T(8,128)(2,1)S(1)}, u32[]{:S(2)}, u32[]{:S(2)}) collective-permute-start(bf16[128,128]{1,0:T(8,128)(2,1)S(1)} %copy.58), channel_id=1, source_target_pairs={{0,12},{4,16},{8,20},{12,24},{16,28},{1,13},{5,17},{9,21},{13,25},... | collective-permute-start | bytes 98312 | tf_op jit(solution)/shard_map/ppermute | solution.py:15
  136.6 1.4 collective-permute-done.11
  138.1 7.6 %scatter_custom_fusion = f32[640,128]{1,0:T(8,128)S(1)} fusion(s32[896]{0:T(1024)S(1)} %bitcast.86, bf16[896,128]{1,0:T(8,128)(2,1)S(1)} %bitcast.83, f32[]{:T(128)} %constant.2.clone.1, pred[896]{0:T(1024)(128)(4,1)S(1)} %bitcast.87), kind=kCustom, calls=%fused_computation.21 | custom fusion | flops 344064 | bytes 559104 | tf_op jit(solution)/shard_map/scatter-add | solution.py:229
  146.4 16.2 %reduce-scatter.7.cloned.1.call-done = bf16[128,4096]{1,0:T(8,128)(2,1)} async-done(((bf16[512,4096]{1,0:T(8,128)(2,1)}), bf16[128,4096]{1,0:T(8,128)(2,1)}) %reduce-scatter.7.cloned.1.call-update) | async-done | bytes 1048592
  162.5 2.3 %copy.42 = bf16[4096,128]{1,0:T(8,128)(2,1)} copy(bf16[4096,128]{0,1:T(8,128)(2,1)} %bitcast.80) | data formatting | bytes 2097152
  (58 shorter events, 5.8 us)
Async XLA Ops:
  7.2 5.7 %copy-start = (bf16[640,128]{1,0:T(8,128)(2,1)S(1)}, bf16[640,128]{1,0:T(8,128)(2,1)}, u32[]{:S(2)}) copy-start(bf16[640,128]{1,0:T(8,128)(2,1)} %param.15) | copy-start | bytes 491524
  7.2 55.5 %all-gather.2.cloned.1.call-start = ((), (), s32[]{:S(2)}) async-start(), calls=%async_computation.2 | async-start | bytes 2293760 | tf_op jit(solution)/shard_map/all_gather | solution.py:203
  12.9 51.4 %copy-start.3 = (bf16[512,128]{1,0:T(8,128)(2,1)S(1)}, bf16[512,128]{1,0:T(8,128)(2,1)}, u32[]{:S(2)}) copy-start(bf16[512,128]{1,0:T(8,128)(2,1)} %param.22) | copy-start | bytes 393220
  15.3 49.4 %copy-start.5 = (bf16[128,512]{1,0:T(8,128)(2,1)S(1)}, bf16[128,512]{1,0:T(8,128)(2,1)}, u32[]{:S(2)}) copy-start(bf16[128,512]{1,0:T(8,128)(2,1)} %param.25) | copy-start | bytes 393220
  15.5 16.5 %collective-permute-start = (bf16[2,128,128]{2,1,0:T(8,128)(2,1)S(1)}, bf16[2,128,128]{2,1,0:T(8,128)(2,1)S(1)}, u32[]{:S(2)}, u32[]{:S(2)}) collective-permute-start(bf16[2,128,128]{2,1,0:T(8,128)(2,1)S(1)} %get-tuple-element.9), channel_id=1, source_target_pairs={{0,12},{4,16},{8,20},{12,24},{16,28},{1,13},{5,17},{9,21},{13,25},... | collective-permute-start | bytes 196616 | tf_op jit(solution)/shard_map/ppermute | solution.py:15
  21.5 19.2 %collective-permute-start.5 = (bf16[2,128,128]{2,1,0:T(8,128)(2,1)S(1)}, bf16[2,128,128]{2,1,0:T(8,128)(2,1)S(1)}, u32[]{:S(2)}, u32[]{:S(2)}) collective-permute-start(bf16[2,128,128]{2,1,0:T(8,128)(2,1)S(1)} %get-tuple-element.8), channel_id=1, source_target_pairs={{12,0},{16,4},{20,8},{24,12},{28,16},{13,1},{17,5},{21,9},{25,13},... | collective-permute-start | bytes 196616 | tf_op jit(solution)/shard_map/ppermute | solution.py:15
  22.8 10.6 %collective-permute-start.1 = (bf16[2,128,128]{2,1,0:T(8,128)(2,1)S(1)}, bf16[2,128,128]{2,1,0:T(8,128)(2,1)S(1)}, u32[]{:S(2)}, u32[]{:S(2)}) collective-permute-start(bf16[2,128,128]{2,1,0:T(8,128)(2,1)S(1)} %get-tuple-element.10), channel_id=1, source_target_pairs={{0,8},{4,12},{8,16},{12,20},{16,24},{20,28},{1,9},{5,13},{9,17},{1... | collective-permute-start | bytes 196616 | tf_op jit(solution)/shard_map/ppermute | solution.py:15
  26.3 7.1 %collective-permute-start.2 = (bf16[2,128,128]{2,1,0:T(8,128)(2,1)S(1)}, bf16[2,128,128]{2,1,0:T(8,128)(2,1)S(1)}, u32[]{:S(2)}, u32[]{:S(2)}) collective-permute-start(bf16[2,128,128]{2,1,0:T(8,128)(2,1)S(1)} %get-tuple-element.11), channel_id=1, source_target_pairs={{0,4},{4,8},{8,12},{12,16},{16,20},{20,24},{24,28},{1,5},{5,9},{9,... | collective-permute-start | bytes 196616 | tf_op jit(solution)/shard_map/ppermute | solution.py:15
  30.7 6.6 %collective-permute-start.3 = (bf16[2,128,128]{2,1,0:T(8,128)(2,1)S(1)}, bf16[2,128,128]{2,1,0:T(8,128)(2,1)S(1)}, u32[]{:S(2)}, u32[]{:S(2)}) collective-permute-start(bf16[2,128,128]{2,1,0:T(8,128)(2,1)S(1)} %get-tuple-element.12), channel_id=1, source_target_pairs={{4,0},{8,4},{12,8},{16,12},{20,16},{24,20},{28,24},{5,1},{9,5},{13... | collective-permute-start | bytes 196616 | tf_op jit(solution)/shard_map/ppermute | solution.py:15
  32.0 8.6 %collective-permute-start.4 = (bf16[2,128,128]{2,1,0:T(8,128)(2,1)S(1)}, bf16[2,128,128]{2,1,0:T(8,128)(2,1)S(1)}, u32[]{:S(2)}, u32[]{:S(2)}) collective-permute-start(bf16[2,128,128]{2,1,0:T(8,128)(2,1)S(1)} %get-tuple-element.13), channel_id=1, source_target_pairs={{8,0},{12,4},{16,8},{20,12},{24,16},{28,20},{9,1},{13,5},{17,9},{2... | collective-permute-start | bytes 196616 | tf_op jit(solution)/shard_map/ppermute | solution.py:15
  40.7 0.8 copy-start.2
  41.5 73.9 %reduce-scatter.9.cloned.1.call-start = ((), (), s32[]{:S(2)}) async-start(), calls=%async_computation.4 | async-start | bytes 1146880
  87.9 3.4 %copy-start.1 = (bf16[4096,128]{1,0:T(8,128)(2,1)S(1)}, bf16[4096,128]{1,0:T(8,128)(2,1)}, u32[]{:S(2)}) copy-start(bf16[4096,128]{1,0:T(8,128)(2,1)} %get-tuple-element.4) | copy-start | bytes 3145732
  87.9 3.4 %copy-start.4 = (bf16[512,128]{1,0:T(8,128)(2,1)S(1)}, bf16[512,128]{1,0:T(8,128)(2,1)}, u32[]{:S(2)}) copy-start(bf16[512,128]{1,0:T(8,128)(2,1)} %w_send_ref.1) | copy-start | bytes 393220
  91.2 71.3 %reduce-scatter.7.cloned.1.call-start = ((), (), s32[]{:S(2)}) async-start(), calls=%async_computation.3 | async-start | bytes 5242880
  116.4 13.8 %collective-permute-start.6 = (bf16[128,128]{1,0:T(8,128)(2,1)S(1)}, bf16[128,128]{1,0:T(8,128)(2,1)S(1)}, u32[]{:S(2)}, u32[]{:S(2)}) collective-permute-start(bf16[128,128]{1,0:T(8,128)(2,1)S(1)} %copy.52), channel_id=1, source_target_pairs={{12,0},{16,4},{20,8},{24,12},{28,16},{13,1},{17,5},{21,9},{25,13},... | collective-permute-start | bytes 98312 | tf_op jit(solution)/shard_map/ppermute | solution.py:15
  118.4 18.1 %collective-permute-start.7 = (bf16[128,128]{1,0:T(8,128)(2,1)S(1)}, bf16[128,128]{1,0:T(8,128)(2,1)S(1)}, u32[]{:S(2)}, u32[]{:S(2)}) collective-permute-start(bf16[128,128]{1,0:T(8,128)(2,1)S(1)} %copy.53), channel_id=1, source_target_pairs={{8,0},{12,4},{16,8},{20,12},{24,16},{28,20},{9,1},{13,5},{17,9},{2... | collective-permute-start | bytes 98312 | tf_op jit(solution)/shard_map/ppermute | solution.py:15
  119.7 16.8 %collective-permute-start.8 = (bf16[128,128]{1,0:T(8,128)(2,1)S(1)}, bf16[128,128]{1,0:T(8,128)(2,1)S(1)}, u32[]{:S(2)}, u32[]{:S(2)}) collective-permute-start(bf16[128,128]{1,0:T(8,128)(2,1)S(1)} %copy.54), channel_id=1, source_target_pairs={{4,0},{8,4},{12,8},{16,12},{20,16},{24,20},{28,24},{5,1},{9,5},{13... | collective-permute-start | bytes 98312 | tf_op jit(solution)/shard_map/ppermute | solution.py:15
  121.0 15.6 %collective-permute-start.9 = (bf16[128,128]{1,0:T(8,128)(2,1)S(1)}, bf16[128,128]{1,0:T(8,128)(2,1)S(1)}, u32[]{:S(2)}, u32[]{:S(2)}) collective-permute-start(bf16[128,128]{1,0:T(8,128)(2,1)S(1)} %copy.56), channel_id=1, source_target_pairs={{0,4},{4,8},{8,12},{12,16},{16,20},{20,24},{24,28},{1,5},{5,9},{9,... | collective-permute-start | bytes 98312 | tf_op jit(solution)/shard_map/ppermute | solution.py:15
  125.6 11.0 %collective-permute-start.10 = (bf16[128,128]{1,0:T(8,128)(2,1)S(1)}, bf16[128,128]{1,0:T(8,128)(2,1)S(1)}, u32[]{:S(2)}, u32[]{:S(2)}) collective-permute-start(bf16[128,128]{1,0:T(8,128)(2,1)S(1)} %copy.57), channel_id=1, source_target_pairs={{0,8},{4,12},{8,16},{12,20},{16,24},{20,28},{1,9},{5,13},{9,17},{1... | collective-permute-start | bytes 98312 | tf_op jit(solution)/shard_map/ppermute | solution.py:15
  130.2 7.9 %collective-permute-start.11 = (bf16[128,128]{1,0:T(8,128)(2,1)S(1)}, bf16[128,128]{1,0:T(8,128)(2,1)S(1)}, u32[]{:S(2)}, u32[]{:S(2)}) collective-permute-start(bf16[128,128]{1,0:T(8,128)(2,1)S(1)} %copy.58), channel_id=1, source_target_pairs={{0,12},{4,16},{8,20},{12,24},{16,28},{1,13},{5,17},{9,21},{13,25},... | collective-permute-start | bytes 98312 | tf_op jit(solution)/shard_map/ppermute | solution.py:15
Sparse Core Ops, SparseCore 0:
  41.6 21.0 all-gather.1
  91.4 23.9 reduce-scatter.8
  117.9 44.5 reduce-scatter.6

commit v2 on v1

--- a/solution.py
+++ b/solution.py
@@ -9,26 +9,9 @@
 from jax.sharding import PartitionSpec as P
 
 
-def shifted(shard, axis, by):
-    devices = lax.axis_size(axis)
-    pairs = [(i, i + by) for i in range(devices) if 0 <= i + by < devices]
-    return lax.ppermute(shard, axis, pairs)
-
-
 def silu_slope(pre_act):
     sigmoid_value = jax.nn.sigmoid(pre_act)
     return sigmoid_value * (1.0 + pre_act * (1.0 - sigmoid_value))
-
-
-def per_offset(blocks, reach, sign, mover):
-    results = []
-    for offset in range(blocks.shape[0]):
-        amount = sign * (reach - offset)
-        if amount == 0:
-            results.append(blocks[offset])
-        else:
-            results.append(mover(blocks[offset], amount))
-    return jnp.stack(results)
 
 
 def largest_divisor(total, highest):
@@ -163,6 +146,334 @@
     )(senders[:, 0, 0], senders, slots, grid_latent, edge_latent, table, w_send, w_edge, bias.reshape(1, hidden))
 
 
+MESH_ID = pl.DeviceIdType.MESH
+DIMS_NT = (((1,), (1,)), ((), ()))
+
+
+def greet(reach):
+    band = lax.axis_index("band")
+    bands = lax.axis_size("band")
+    part = lax.axis_index("mp")
+    parts = lax.axis_size("mp")
+    barrier = pltpu.get_barrier_semaphore()
+    for turn in range(1, parts):
+        pl.semaphore_signal(
+            barrier, inc=1, device_id=(band, lax.rem(part + turn, parts)), device_id_type=MESH_ID
+        )
+    shifts = [by for by in range(-reach, reach + 1) if by != 0]
+    for by in shifts:
+        @pl.when((band + by >= 0) & (band + by < bands))
+        def _():
+            pl.semaphore_signal(barrier, inc=1, device_id=(band + by, part), device_id_type=MESH_ID)
+
+    below = jnp.minimum(band, reach)
+    above = jnp.minimum(bands - 1 - band, reach)
+    pl.semaphore_wait(barrier, parts - 1 + below + above)
+
+
+def spread_kernel(
+    rows_ref, wanted_ref, w_recv_ref, w_out_ref, rows_w_ref,
+    table_ref, weight_ref,
+    held, both, stage, landed, weight_land,
+    near_send, near_recv, far_send, far_recv, pass_send, pass_recv,
+    band_send, band_recv, weight_send, weight_recv,
+    *, reach,
+):
+    band = lax.axis_index("band")
+    bands = lax.axis_size("band")
+    part = lax.axis_index("mp")
+    parts = lax.axis_size("mp")
+    across = lax.rem(part + parts // 2, parts)
+    beside = part + 1 - 2 * lax.rem(part, 2)
+    span, capacity = wanted_ref.shape
+    node_count, twice = rows_ref.shape
+    cols = twice // 2
+    hidden = w_recv_ref.shape[1]
+    greet(reach)
+
+    def remote(source, target, send, recv, device):
+        return pltpu.make_async_remote_copy(
+            src_ref=source, dst_ref=target, send_sem=send, recv_sem=recv,
+            device_id=device, device_id_type=MESH_ID,
+        )
+
+    far = remote(rows_ref, held.at[part], far_send, far_recv, (band, across))
+    near = remote(rows_ref, held.at[part], near_send, near_recv, (band, beside))
+    far.start()
+    near.start()
+    weight_rows = rows_w_ref.shape[0] // parts
+    moves = []
+    for turn in range(1, parts):
+        peer = lax.rem(part + turn, parts)
+        move = remote(
+            rows_w_ref.at[pl.ds(pl.multiple_of(peer * weight_rows, weight_rows), weight_rows), :],
+            weight_land.at[part], weight_send.at[turn], weight_recv.at[turn], (band, peer),
+        )
+        move.start()
+        moves.append(move)
+    weight_land[part] = rows_w_ref[
+        pl.ds(pl.multiple_of(part * weight_rows, weight_rows), weight_rows), :
+    ]
+    held[part] = rows_ref[...]
+    far.wait_recv()
+    onward = remote(held.at[across], held.at[across], pass_send, pass_recv, (band, beside))
+    onward.start()
+    near.wait_recv()
+    onward.wait_recv()
+    ahead = jnp.zeros((node_count, hidden), jnp.float32)
+    back = jnp.zeros((node_count, hidden), jnp.float32)
+    for j in range(held.shape[0]):
+        block = held[j]
+        ahead += jnp.dot(
+            block[:, :cols], w_recv_ref[j * cols : (j + 1) * cols, :],
+            preferred_element_type=jnp.float32,
+        )
+        back += lax.dot_general(
+            block[:, cols:], w_out_ref[:, j * cols : (j + 1) * cols], DIMS_NT,
+            preferred_element_type=jnp.float32,
+        )
+    both[:, :hidden] = ahead.astype(both.dtype)
+    both[:, hidden:] = back.astype(both.dtype)
+    lanes = lax.broadcasted_iota(jnp.int32, (capacity, 128), 1).astype(jnp.float32)
+    order = sorted(range(span), key=lambda k: -abs(k - reach))
+    sends = {}
+    for k in order:
+        row = wanted_ref[k : k + 1, :].astype(jnp.float32)
+        column = jnp.broadcast_to(row, (128, capacity)).T
+        pick = jnp.concatenate(
+            [
+                jnp.where(column - 128.0 * j == lanes, 1.0, 0.0).astype(jnp.bfloat16)
+                for j in range(node_count // 128)
+            ],
+            axis=1,
+        )
+        chosen = jnp.dot(pick, both[...], preferred_element_type=jnp.float32).astype(jnp.bfloat16)
+        if k == reach:
+            landed[k] = chosen
+            continue
+        stage[k] = chosen
+        target = band + reach - k
+        sends[k] = remote(
+            stage.at[k], landed.at[k], band_send.at[k], band_recv.at[k], (target, part)
+        )
+
+        @pl.when((target >= 0) & (target < bands))
+        def _():
+            sends[k].start()
+
+        source = band + k - reach
+
+        @pl.when((source < 0) | (source >= bands))
+        def _():
+            landed[k] = jnp.zeros((capacity, 2 * hidden), landed.dtype)
+
+    for move in moves:
+        move.wait_recv()
+    weight_ref[...] = weight_land[...]
+    for k in reversed(order):
+        if k == reach:
+            continue
+        source = band + k - reach
+
+        @pl.when((source >= 0) & (source < bands))
+        def _():
+            sends[k].wait_recv()
+
+    table_ref[...] = landed[...].reshape(span * capacity, 2 * hidden)
+    far.wait_send()
+    near.wait_send()
+    onward.wait_send()
+    for move in moves:
+        move.wait_send()
+    for k in order:
+        if k == reach:
+            continue
+        target = band + reach - k
+
+        @pl.when((target >= 0) & (target < bands))
+        def _():
+            sends[k].wait_send()
+
+
+VMEM_SPEC = pl.BlockSpec(memory_space=pltpu.VMEM)
+DMA_SEM = pltpu.SemaphoreType.DMA
+
+
+def spread(rows, wanted, w_recv, w_out, rows_w, parts, reach):
+    span, capacity = wanted.shape
+    node_count, twice = rows.shape
+    hidden = w_recv.shape[1]
+    weight_shape = (parts, rows_w.shape[0] // parts, rows_w.shape[1])
+    return pl.pallas_call(
+        functools.partial(spread_kernel, reach=reach),
+        in_specs=[VMEM_SPEC] * 5,
+        out_specs=[VMEM_SPEC] * 2,
+        out_shape=[
+            jax.ShapeDtypeStruct((span * capacity, 2 * hidden), jnp.bfloat16),
+            jax.ShapeDtypeStruct(weight_shape, jnp.bfloat16),
+        ],
+        scratch_shapes=[
+            pltpu.VMEM((parts, node_count, twice), jnp.bfloat16),
+            pltpu.VMEM((node_count, 2 * hidden), jnp.bfloat16),
+            pltpu.VMEM((span, capacity, 2 * hidden), jnp.bfloat16),
+            pltpu.VMEM((span, capacity, 2 * hidden), jnp.bfloat16),
+            pltpu.VMEM(weight_shape, jnp.bfloat16),
+        ]
+        + [DMA_SEM] * 6
+        + [DMA_SEM((span,)), DMA_SEM((span,)), DMA_SEM((parts,)), DMA_SEM((parts,))],
+        compiler_params=pltpu.CompilerParams(collective_id=0, has_side_effects=True),
+        name="spread",
+    )(rows, wanted, w_recv, w_out, rows_w)
+
+
+def collect_kernel(
+    slot_ref, sender_ref, wanted_ref, weight_ref,
+    grid_ref, node_ref,
+    back, held, node_stage, node_held,
+    band_send, band_recv, near_send, near_recv, far_send, far_recv, pass_send, pass_recv,
+    *, reach, chunks,
+):
+    band = lax.axis_index("band")
+    bands = lax.axis_size("band")
+    part = lax.axis_index("mp")
+    parts = lax.axis_size("mp")
+    across = lax.rem(part + parts // 2, parts)
+    beside = part + 1 - 2 * lax.rem(part, 2)
+    span, capacity = wanted_ref.shape
+    node_count, hidden = node_stage.shape
+    rows = sender_ref.shape[0] // chunks
+    greet(reach)
+
+    def remote(source, target, send, recv, device):
+        return pltpu.make_async_remote_copy(
+            src_ref=source, dst_ref=target, send_sem=send, recv_sem=recv,
+            device_id=device, device_id_type=MESH_ID,
+        )
+
+    order = [k for k in sorted(range(span), key=lambda k: -abs(k - reach)) if k != reach]
+    sends = {}
+    for k in order:
+        target = band + k - reach
+        sends[k] = remote(
+            slot_ref.at[k], back.at[k], band_send.at[k], band_recv.at[k], (target, part)
+        )
+
+        @pl.when((target >= 0) & (target < bands))
+        def _():
+            sends[k].start()
+
+    def slab(index):
+        return pl.ds(index * rows, rows)
+
+    fars, nears, onwards = [], [], []
+    for c in range(chunks):
+        source = sender_ref.at[slab(c), :]
+        fars.append(
+            remote(source, held.at[part, slab(c), :], far_send.at[c], far_recv.at[c], (band, across))
+        )
+        nears.append(
+            remote(source, held.at[part, slab(c), :], near_send.at[c], near_recv.at[c], (band, beside))
+        )
+        fars[c].start()
+        nears[c].start()
+    held[part] = sender_ref[...]
+
+    def node_row(k):
+        ids = lax.broadcasted_iota(jnp.int32, (node_count, capacity), 0)
+        return jnp.where(ids == wanted_ref[k : k + 1, :], 1.0, 0.0).astype(jnp.bfloat16)
+
+    node_sum = jnp.dot(node_row(reach), slot_ref[reach], preferred_element_type=jnp.float32)
+    for k in reversed(order):
+        source = band + reach - k
+
+        @pl.when((source >= 0) & (source < bands))
+        def _():
+            sends[k].wait_recv()
+
+        @pl.when((source < 0) | (source >= bands))
+        def _():
+            back[k] = jnp.zeros((capacity, hidden), back.dtype)
+
+        node_sum += jnp.dot(node_row(k), back[k], preferred_element_type=jnp.float32)
+    node_stage[...] = node_sum.astype(node_stage.dtype)
+    node_held[part] = node_sum.astype(node_held.dtype)
+    fars.append(
+        remote(node_stage, node_held.at[part], far_send.at[chunks], far_recv.at[chunks], (band, across))
+    )
+    nears.append(
+        remote(node_stage, node_held.at[part], near_send.at[chunks], near_recv.at[chunks], (band, beside))
+    )
+    fars[chunks].start()
+    nears[chunks].start()
+
+    def pass_on(c):
+        fars[c].wait_recv()
+        block = held.at[across, slab(c), :] if c < chunks else node_held.at[across]
+        onwards.append(remote(block, block, pass_send.at[c], pass_recv.at[c], (band, beside)))
+        onwards[c].start()
+
+    def finish(c):
+        nears[c].wait_recv()
+        onwards[c].wait_recv()
+        if c < chunks:
+            blocks = [held[j, c * rows : (c + 1) * rows, :] for j in range(held.shape[0])]
+            weights = [weight_ref[j, :, :hidden] for j in range(held.shape[0])]
+        else:
+            blocks = [node_held[j] for j in range(held.shape[0])]
+            weights = [weight_ref[j, :, hidden:] for j in range(held.shape[0])]
+        total = lax.dot_general(
+            jnp.concatenate(blocks, axis=1), jnp.concatenate(weights, axis=1), DIMS_NT,
+            preferred_element_type=jnp.float32,
+        )
+        if c < chunks:
+            grid_ref[c * rows : (c + 1) * rows, :] = total.astype(grid_ref.dtype)
+        else:
+            node_ref[...] = total.astype(node_ref.dtype)
+
+    for c in range(chunks + 1):
+        pass_on(c)
+        if c > 0:
+            finish(c - 1)
+    finish(chunks)
+    for c in range(chunks + 1):
+        fars[c].wait_send()
+        nears[c].wait_send()
+        onwards[c].wait_send()
+    for k in order:
+        target = band + k - reach
+
+        @pl.when((target >= 0) & (target < bands))
+        def _():
+            sends[k].wait_send()
+
+
+def collect(slot_sum, sender_sum, wanted, weights, node_count, reach):
+    span, capacity = wanted.shape
+    grid_rows, hidden = sender_sum.shape
+    parts, out_cols, _ = weights.shape
+    chunks = 4
+    tokens = chunks + 1
+    return pl.pallas_call(
+        functools.partial(collect_kernel, reach=reach, chunks=chunks),
+        in_specs=[VMEM_SPEC] * 4,
+        out_specs=[VMEM_SPEC] * 2,
+        out_shape=[
+            jax.ShapeDtypeStruct((grid_rows, out_cols), jnp.bfloat16),
+            jax.ShapeDtypeStruct((node_count, out_cols), jnp.bfloat16),
+        ],
+        scratch_shapes=[
+            pltpu.VMEM((span, capacity, hidden), jnp.bfloat16),
+            pltpu.VMEM((parts, grid_rows, hidden), jnp.bfloat16),
+            pltpu.VMEM((node_count, hidden), jnp.bfloat16),
+            pltpu.VMEM((parts, node_count, hidden), jnp.bfloat16),
+        ]
+        + [DMA_SEM((span,))] * 2
+        + [DMA_SEM((tokens,))] * 6,
+        compiler_params=pltpu.CompilerParams(collective_id=1, has_side_effects=True),
+        name="collect",
+    )(slot_sum.reshape(span, capacity, hidden), sender_sum, wanted, weights)
+
+
 def per_device(
     grid_latent,
     edge_latent,
@@ -179,61 +490,25 @@
     w_out,
 ):
     span = request.shape[1]
-    capacity = request.shape[2]
     reach = (span - 1) // 2
-    node_count = mesh_latent.shape[0]
-    latent = grid_latent.shape[1]
-    slot_count = span * capacity
+    parts = lax.axis_size("mp")
     scaled_grad = (mesh_grad.astype(jnp.float32) / counts.astype(jnp.float32)[:, None]).astype(
         jnp.bfloat16
     )
     wanted = request[0]
-    live_slot = (wanted >= 0)[:, :, None]
-    picker = jnp.maximum(wanted, 0)
-    flat_live = live_slot.reshape(slot_count, 1)
-    flat_picker = picker.reshape(-1)
-    send_both = jnp.stack(
-        [
-            jnp.where(live_slot, mesh_latent[picker], 0),
-            jnp.where(live_slot, scaled_grad[picker], 0),
-        ],
-        axis=1,
-    )
-    got_part = per_offset(send_both, reach, 1, lambda block, amount: shifted(block, "band", amount))
-    got = lax.all_gather(got_part, "mp", axis=3, tiled=True)
-    slot_proj = jnp.dot(
-        got[:, 0].reshape(slot_count, latent), w_recv, preferred_element_type=jnp.float32
-    )
-    slot_back = jnp.dot(
-        got[:, 1].reshape(slot_count, latent), w_out.T, preferred_element_type=jnp.float32
-    )
-    table = jnp.concatenate([slot_proj, slot_back], axis=1).astype(jnp.bfloat16)
+    table, weights = spread(
+        jnp.concatenate([mesh_latent, scaled_grad], axis=1),
+        wanted,
+        w_recv,
+        w_out,
+        jnp.concatenate([w_send, w_recv], axis=1),
+        parts,
+        reach,
+    )
     sender_sum, slot_sum = edge_pass(
-        grid_latent, edge_latent, table, edge_sender, edge_slot, w_send, w_edge, edge_bias, jnp.float32
-    )
-    recv_wide = w_recv.astype(jnp.float32)
-    slot_term = jnp.dot(slot_sum, recv_wide.T, precision=lax.Precision.HIGHEST)
-    slot_share = lax.psum_scatter(
-        slot_term.astype(jnp.bfloat16), "mp", scatter_dimension=1, tiled=True
-    ).astype(jnp.float32)
-    part_cols = slot_share.shape[1]
-    returned = per_offset(
-        slot_share.reshape(span, capacity, part_cols),
-        reach,
-        -1,
-        lambda block, amount: shifted(block.astype(jnp.bfloat16), "band", amount).astype(
-            block.dtype
-        ),
-    )
-    kept_rows = jnp.where(flat_live, returned.reshape(slot_count, part_cols), 0.0)
-    node_grad = jax.ops.segment_sum(kept_rows, flat_picker, num_segments=node_count).astype(
-        jnp.bfloat16
-    )
-    grid_term = jnp.dot(sender_sum, w_send.T, preferred_element_type=jnp.float32)
-    grid_grad = lax.psum_scatter(
-        grid_term.astype(jnp.bfloat16), "mp", scatter_dimension=1, tiled=True
-    )
-    return (grid_grad, node_grad)
+        grid_latent, edge_latent, table, edge_sender, edge_slot, w_send, w_edge, edge_bias, jnp.bfloat16
+    )
+    return tuple(collect(slot_sum, sender_sum, wanted, weights, mesh_latent.shape[0], reach))
 
 
 def solution(mesh):

time: 172 us -> 94.7 us (0.55)
  Pallas kernels: 22 us -> 81.6 us
  waiting for transfers between devices: 58.9 us -> 0 us
  starting transfers between devices: 37.2 us -> 0 us
  local copies, waits for them, and re-layouts: 20.6 us -> 6.66 us
  between operations: 14.2 us -> 0.66 us
  other arithmetic: 12.5 us -> 5.16 us
  matrix products: 6.01 us -> 0 us
    pallas_call x0 -> x2, Pallas kernels: none -> 59.7 us  [the longest x1 35.6 us: collect(): pl.pallas_call(functools.partial(collect_kernel, reach=reach, chunks=chun...]
    ppermute x12 -> x0, starting transfers between devices: 37 us -> none  [shifted(): return lax.ppermute(shard, axis, pairs)]
    unnamed x5 -> x0, waiting for transfers between devices: 30.6 us -> none
    all_gather x1 -> x0, waiting for transfers between devices: 19.6 us -> none  [per_device(): got = lax.all_gather(got_part, 'mp', axis=3, tiled=True)]
    ppermute x12 -> x0, waiting for transfers between devices: 8.71 us -> none  [shifted(): return lax.ppermute(shard, axis, pairs)]
    scatter-add x1 -> x0, other arithmetic: 7.59 us -> none  [per_device(): jax.ops.segment_sum(kept_rows, flat_picker, num_segments=node_count)]
    unnamed x34 -> x3, local copies, waits for them, and re-layouts: 11.8 us -> 5.13 us
    dot_general x4 -> x0, matrix products: 6.01 us -> none  [the longest x1 3.22 us: per_device(): jnp.dot(sender_sum, w_send.T, preferred_element_type=jnp.float32)]
  transfers between devices with their start and end apart: 15 -> 0, of which waited for: 6 -> 0; matrix products, arithmetic and copies ran while one was open for 12% -> 0% of each run, Pallas kernels for 0% -> 0%
where the time goes in v2:
time: 94.7 us; the launch traced here: 94.1 us
  Pallas kernels  81.6 us (86%)
  local copies, waits for them, and re-layouts  6.66 us (7%)
  other arithmetic  5.16 us (5%)
    pallas_call x1, Pallas kernels, collect(): pl.pallas_call(functools.partial(collect_kernel, reach=reach, chunks=chun...  35.6 us
    pallas_call x1, Pallas kernels, spread(): pl.pallas_call(functools.partial(spread_kernel, reach=reach), in_specs=[V...  24 us
    pallas_call x1, Pallas kernels, edge_pass(): pl.pallas_call(functools.partial(edge_kernel, grid_blocks=grid_blocks, gr...  22 us
    unnamed x3, local copies, waits for them, and re-layouts  5.13 us

profile of v2, /device:TPU:0, one launch (start us, length us, event | category | flops | bytes accessed | tf_op | source)
XLA Modules:
  0.0 94.1 jit_solution(5308374989425504806)
XLA Ops:
  0.6 1.5 %slice_reduce_fusion.anchors = s32[12]{0:T(128)} fusion(s32[12,1,512]{2,1,0:T(1,128)} %bitcast.10), kind=kLoop, calls=%fused_computation.3 | loop fusion | bytes 96 | tf_op jit(solution)/shard_map/slice | solution.py:146
  2.2 0.7 convert_element_type.10
  2.8 1.3 %copy.17 = s32[1,7,128]{2,1,0:T(8,128)} copy(s32[1,7,128]{2,0,1:T(1,128)} %param.18) | data formatting | bytes 7168
  4.1 1.1 %divide_convert_fusion = bf16[640,128]{1,0:T(8,128)(2,1)S(1)} fusion(bf16[640,128]{1,0:T(8,128)(2,1)} %param.16, f32[640]{0:T(1024)S(1)} %convert_element_type.10), kind=kLoop, calls=%fused_computation.1 | loop fusion | flops 245760 | bytes 330240 | tf_op jit(solution)/shard_map/convert_element_type | solution.py:495
  5.2 1.7 %pad_maximum_fusion.rows_ref = bf16[640,256]{1,0:T(8,128)(2,1)} fusion(bf16[640,128]{1,0:T(8,128)(2,1)S(1)} %divide_convert_fusion, bf16[640,128]{1,0:T(8,128)(2,1)} %param.15), kind=kLoop, calls=%fused_computation | loop fusion | flops 655360 | bytes 655360 | tf_op jit(solution)/shard_map/concatenate | solution.py:500
  6.9 1.7 %pad_maximum_fusion.1.rows_w_ref = bf16[512,256]{1,0:T(8,128)(2,1)} fusion(bf16[512,128]{1,0:T(8,128)(2,1)} %w_recv_ref.1, bf16[512,128]{1,0:T(8,128)(2,1)} %w_send_ref.1), kind=kLoop, calls=%fused_computation.2 | loop fusion | flops 524288 | bytes 524288 | tf_op jit(solution)/shard_map/concatenate | solution.py:504
  8.6 24.0 %spread.1 = (bf16[896,256]{1,0:T(8,128)(2,1)}, bf16[4,128,256]{2,1,0:T(8,128)(2,1)}) custom-call(bf16[640,256]{1,0:T(8,128)(2,1)} %pad_maximum_fusion.rows_ref, s32[7,128]{1,0:T(8,128)} %bitcast.8, bf16[512,128]{1,0:T(8,128)(2,1)} %w_recv_ref.1, bf16[128,512]{1,0:T(8,128)(2,1)} %w_out_ref.1, bf16[512,256]{1,0:T(8,128)(2,1)} %pad_maximum_fusion.1.rows_w_ref), custom_call_target="tpu_custom_call" | custom-call | tf_op jit(solution)/shard_map/spread/pallas_call | solution.py:307
  32.6 22.0 %edge_pass.1 = (bf16[4096,128]{1,0:T(8,128)(2,1)}, bf16[896,128]{1,0:T(8,128)(2,1)}) custom-call(s32[12]{0:T(128)} %slice_reduce_fusion.anchors, s32[12,1,512]{2,1,0:T(1,128)} %bitcast.11, s32[12,1,512]{2,1,0:T(1,128)} %bitcast.12, bf16[4096,512]{1,0:T(8,128)(2,1)} %grid_ref.1, bf16[6144,512]{1,0:T(8,128)(2,1)} %edge_ref.1, ...), custom_call_target="tpu_custom_call" | custom-call | flops 10000000000 | bytes 12000000 | tf_op jit(solution)/shard_map/edge_pass/pallas_call | solution.py:110
  54.6 35.6 %collect.1 = (bf16[4096,128]{1,0:T(8,128)(2,1)}, bf16[640,128]{1,0:T(8,128)(2,1)}) custom-call(bf16[7,128,128]{2,1,0:T(8,128)(2,1)} %bitcast.7, bf16[4096,128]{1,0:T(8,128)(2,1)} %get-tuple-element.8.sender_ref, s32[7,128]{1,0:T(8,128)} %bitcast.9, bf16[4,128,256]{2,1,0:T(8,128)(2,1)} %get-tuple-element.9.weight_ref), custom_call_target="tpu_custom_call" | custom-call | tf_op jit(solution)/shard_map/collect/pallas_call | solution.py:456
  90.2 2.3 %copy.20 = bf16[4096,128]{1,0:T(8,128)(2,1)} copy(bf16[4096,128]{1,0:T(8,128)(2,1)} %get-tuple-element.12) | data formatting | bytes 2097152
  92.5 1.6 %copy.21 = bf16[640,128]{1,0:T(8,128)(2,1)} copy(bf16[640,128]{1,0:T(8,128)(2,1)} %get-tuple-element.13) | data formatting | bytes 327680

commit v3 on v2

--- a/solution.py
+++ b/solution.py
@@ -58,7 +58,7 @@
             grid_ref[...], w_send_ref[...], preferred_element_type=jnp.float32
         )
 
-    anchor = anchors[step]
+    anchor = anchors[step * width]
     local = sender_ref[0].astype(jnp.float32) - anchor.astype(jnp.float32)
     slots = slot_ref[0].astype(jnp.float32)
     lanes = lax.broadcasted_iota(jnp.int32, (width, 128), 1).astype(jnp.float32)
@@ -143,7 +143,7 @@
             flops=10_000_000_000, bytes_accessed=12_000_000, transcendentals=0
         ),
         name="edge_pass",
-    )(senders[:, 0, 0], senders, slots, grid_latent, edge_latent, table, w_send, w_edge, bias.reshape(1, hidden))
+    )(edge_sender, senders, slots, grid_latent, edge_latent, table, w_send, w_edge, bias.reshape(1, hidden))
 
 
 MESH_ID = pl.DeviceIdType.MESH
@@ -172,7 +172,7 @@
 
 
 def spread_kernel(
-    rows_ref, wanted_ref, w_recv_ref, w_out_ref, rows_w_ref,
+    latent_ref, grad_ref, counts_ref, wanted_ref, w_recv_ref, w_out_ref, w_send_ref,
     table_ref, weight_ref,
     held, both, stage, landed, weight_land,
     near_send, near_recv, far_send, far_recv, pass_send, pass_recv,
@@ -186,9 +186,16 @@
     across = lax.rem(part + parts // 2, parts)
     beside = part + 1 - 2 * lax.rem(part, 2)
     span, capacity = wanted_ref.shape
-    node_count, twice = rows_ref.shape
-    cols = twice // 2
+    node_count, cols = latent_ref.shape
     hidden = w_recv_ref.shape[1]
+    count_row = counts_ref[...].astype(jnp.float32)
+    count_col = jnp.broadcast_to(count_row, (cols, node_count)).T
+    held[part, :, :cols] = latent_ref[...]
+    held[part, :, cols:] = (grad_ref[...].astype(jnp.float32) / count_col).astype(held.dtype)
+    weight_rows = w_send_ref.shape[0] // parts
+    own_rows = pl.ds(pl.multiple_of(part * weight_rows, weight_rows), weight_rows)
+    weight_land[0, part] = w_send_ref[own_rows, :]
+    weight_land[1, part] = w_recv_ref[own_rows, :]
     greet(reach)
 
     def remote(source, target, send, recv, device):
@@ -197,24 +204,21 @@
             device_id=device, device_id_type=MESH_ID,
         )
 
-    far = remote(rows_ref, held.at[part], far_send, far_recv, (band, across))
-    near = remote(rows_ref, held.at[part], near_send, near_recv, (band, beside))
+    far = remote(held.at[part], held.at[part], far_send, far_recv, (band, across))
+    near = remote(held.at[part], held.at[part], near_send, near_recv, (band, beside))
     far.start()
     near.start()
-    weight_rows = rows_w_ref.shape[0] // parts
     moves = []
     for turn in range(1, parts):
         peer = lax.rem(part + turn, parts)
-        move = remote(
-            rows_w_ref.at[pl.ds(pl.multiple_of(peer * weight_rows, weight_rows), weight_rows), :],
-            weight_land.at[part], weight_send.at[turn], weight_recv.at[turn], (band, peer),
-        )
-        move.start()
-        moves.append(move)
-    weight_land[part] = rows_w_ref[
-        pl.ds(pl.multiple_of(part * weight_rows, weight_rows), weight_rows), :
-    ]
-    held[part] = rows_ref[...]
+        peer_rows = pl.ds(pl.multiple_of(peer * weight_rows, weight_rows), weight_rows)
+        for which, ref in enumerate((w_send_ref, w_recv_ref)):
+            move = remote(
+                ref.at[peer_rows, :], weight_land.at[which, part],
+                weight_send.at[which, turn], weight_recv.at[which, turn], (band, peer),
+            )
+            move.start()
+            moves.append(move)
     far.wait_recv()
     onward = remote(held.at[across], held.at[across], pass_send, pass_recv, (band, beside))
     onward.start()
@@ -299,31 +303,31 @@
 DMA_SEM = pltpu.SemaphoreType.DMA
 
 
-def spread(rows, wanted, w_recv, w_out, rows_w, parts, reach):
+def spread(mesh_latent, mesh_grad, counts, wanted, w_recv, w_out, w_send, parts, reach):
     span, capacity = wanted.shape
-    node_count, twice = rows.shape
+    node_count, cols = mesh_latent.shape
     hidden = w_recv.shape[1]
-    weight_shape = (parts, rows_w.shape[0] // parts, rows_w.shape[1])
+    weight_shape = (2, parts, w_send.shape[0] // parts, hidden)
     return pl.pallas_call(
         functools.partial(spread_kernel, reach=reach),
-        in_specs=[VMEM_SPEC] * 5,
+        in_specs=[VMEM_SPEC] * 7,
         out_specs=[VMEM_SPEC] * 2,
         out_shape=[
             jax.ShapeDtypeStruct((span * capacity, 2 * hidden), jnp.bfloat16),
             jax.ShapeDtypeStruct(weight_shape, jnp.bfloat16),
         ],
         scratch_shapes=[
-            pltpu.VMEM((parts, node_count, twice), jnp.bfloat16),
+            pltpu.VMEM((parts, node_count, 2 * cols), jnp.bfloat16),
             pltpu.VMEM((node_count, 2 * hidden), jnp.bfloat16),
             pltpu.VMEM((span, capacity, 2 * hidden), jnp.bfloat16),
             pltpu.VMEM((span, capacity, 2 * hidden), jnp.bfloat16),
             pltpu.VMEM(weight_shape, jnp.bfloat16),
         ]
         + [DMA_SEM] * 6
-        + [DMA_SEM((span,)), DMA_SEM((span,)), DMA_SEM((parts,)), DMA_SEM((parts,))],
+        + [DMA_SEM((span,)), DMA_SEM((span,)), DMA_SEM((2, parts)), DMA_SEM((2, parts))],
         compiler_params=pltpu.CompilerParams(collective_id=0, has_side_effects=True),
         name="spread",
-    )(rows, wanted, w_recv, w_out, rows_w)
+    )(mesh_latent, mesh_grad, counts.reshape(1, node_count), wanted, w_recv, w_out, w_send)
 
 
 def collect_kernel(
@@ -417,10 +421,10 @@
         onwards[c].wait_recv()
         if c < chunks:
             blocks = [held[j, c * rows : (c + 1) * rows, :] for j in range(held.shape[0])]
-            weights = [weight_ref[j, :, :hidden] for j in range(held.shape[0])]
+            weights = [weight_ref[0, j] for j in range(held.shape[0])]
         else:
             blocks = [node_held[j] for j in range(held.shape[0])]
-            weights = [weight_ref[j, :, hidden:] for j in range(held.shape[0])]
+            weights = [weight_ref[1, j] for j in range(held.shape[0])]
         total = lax.dot_general(
             jnp.concatenate(blocks, axis=1), jnp.concatenate(weights, axis=1), DIMS_NT,
             preferred_element_type=jnp.float32,
@@ -450,7 +454,7 @@
 def collect(slot_sum, sender_sum, wanted, weights, node_count, reach):
     span, capacity = wanted.shape
     grid_rows, hidden = sender_sum.shape
-    parts, out_cols, _ = weights.shape
+    _, parts, out_cols, _ = weights.shape
     chunks = 4
     tokens = chunks + 1
     return pl.pallas_call(
@@ -492,18 +496,9 @@
     span = request.shape[1]
     reach = (span - 1) // 2
     parts = lax.axis_size("mp")
-    scaled_grad = (mesh_grad.astype(jnp.float32) / counts.astype(jnp.float32)[:, None]).astype(
-        jnp.bfloat16
-    )
     wanted = request[0]
     table, weights = spread(
-        jnp.concatenate([mesh_latent, scaled_grad], axis=1),
-        wanted,
-        w_recv,
-        w_out,
-        jnp.concatenate([w_send, w_recv], axis=1),
-        parts,
-        reach,
+        mesh_latent, mesh_grad, counts, wanted, w_recv, w_out, w_send, parts, reach
     )
     sender_sum, slot_sum = edge_pass(
         grid_latent, edge_latent, table, edge_sender, edge_slot, w_send, w_edge, edge_bias, jnp.bfloat16

time: 94.7 us -> 89.8 us (0.948)
  other arithmetic: 5.16 us -> 0 us
    concatenate x2 -> x0, other arithmetic: 3.4 us -> none  [the longest x1 1.71 us: per_device(): jnp.concatenate([w_send, w_recv], axis=1)]
    convert_element_type x2 -> x0, other arithmetic: 1.76 us -> none  [the longest x1 1.07 us: per_device(): (mesh_grad.astype(jnp.float32) / counts.astype(jnp.float32)[:, None]).ast...]
    slice x1 -> x0, local copies, waits for them, and re-layouts: 1.53 us -> none  [edge_pass(): senders[:, 0, 0]]
    reshape x0 -> x1, local copies, waits for them, and re-layouts: none -> 1.27 us  [spread(): counts.reshape(1, node_count)]
where the time goes in v3:
time: 89.8 us; the launch traced here: 89.2 us
  Pallas kernels  82.2 us (92%)
  local copies, waits for them, and re-layouts  6.4 us (7%)
    pallas_call x1, Pallas kernels, collect(): pl.pallas_call(functools.partial(collect_kernel, reach=reach, chunks=chun...  35.6 us
    pallas_call x1, Pallas kernels, spread(): pl.pallas_call(functools.partial(spread_kernel, reach=reach), in_specs=[V...  24.3 us
    pallas_call x1, Pallas kernels, edge_pass(): pl.pallas_call(functools.partial(edge_kernel, grid_blocks=grid_blocks, gr...  22.2 us
    unnamed x3, local copies, waits for them, and re-layouts  5.13 us

profile of v3, /device:TPU:0, one launch (start us, length us, event | category | flops | bytes accessed | tf_op | source)
XLA Modules:
  0.0 89.2 jit_solution(2347232354441767067)
XLA Ops:
  0.6 1.3 %reshape.21.counts_ref = s32[1,640]{1,0:T(1,128)} reshape(s32[640]{0:T(1024)} %param.17) | data formatting | bytes 5120 | tf_op jit(solution)/shard_map/reshape | solution.py:330
  1.9 1.3 %copy.17 = s32[1,7,128]{2,1,0:T(8,128)} copy(s32[1,7,128]{2,0,1:T(1,128)} %param.18) | data formatting | bytes 7168
  3.2 24.3 %spread.1 = (bf16[896,256]{1,0:T(8,128)(2,1)}, bf16[2,4,128,128]{3,2,1,0:T(8,128)(2,1)}) custom-call(bf16[640,128]{1,0:T(8,128)(2,1)} %latent_ref.1, bf16[640,128]{1,0:T(8,128)(2,1)} %grad_ref.1, s32[1,640]{1,0:T(1,128)} %reshape.21.counts_ref, s32[7,128]{1,0:T(8,128)} %bitcast.8, bf16[512,128]{1,0:T(8,128)(2,1)} %w_recv_ref.1, bf16[128,512]{1,0:T(8,128)(2,1)} %w_out_ref.1, ...), custom_call_target="tpu_custom_call" | custom-call | tf_op jit(solution)/shard_map/spread/pallas_call | solution.py:311
  27.5 22.2 %edge_pass.1 = (bf16[4096,128]{1,0:T(8,128)(2,1)}, bf16[896,128]{1,0:T(8,128)(2,1)}) custom-call(s32[6144]{0:T(1024)} %anchors.1, s32[12,1,512]{2,1,0:T(1,128)} %bitcast.10, s32[12,1,512]{2,1,0:T(1,128)} %bitcast.11, bf16[4096,512]{1,0:T(8,128)(2,1)} %grid_ref.1, bf16[6144,512]{1,0:T(8,128)(2,1)} %edge_ref.1, bf16[896,256]{1,0:T(8,128)(2,1)} %get-tuple-element.6.table_ref, ...), custom_call_target="tpu_custom_call" | custom-call | flops 10000000000 | bytes 12000000 | tf_op jit(solution)/shard_map/edge_pass/pallas_call | solution.py:110
  49.7 35.6 %collect.1 = (bf16[4096,128]{1,0:T(8,128)(2,1)}, bf16[640,128]{1,0:T(8,128)(2,1)}) custom-call(bf16[7,128,128]{2,1,0:T(8,128)(2,1)} %bitcast.7, bf16[4096,128]{1,0:T(8,128)(2,1)} %get-tuple-element.8.sender_ref, s32[7,128]{1,0:T(8,128)} %bitcast.9, bf16[2,4,128,128]{3,2,1,0:T(8,128)(2,1)} %get-tuple-element.9.weight_ref), custom_call_target="tpu_custom_call" | custom-call | tf_op jit(solution)/shard_map/collect/pallas_call | solution.py:460
  85.4 2.3 %copy.20 = bf16[4096,128]{1,0:T(8,128)(2,1)} copy(bf16[4096,128]{1,0:T(8,128)(2,1)} %get-tuple-element.12) | data formatting | bytes 2097152
  87.6 1.6 %copy.21 = bf16[640,128]{1,0:T(8,128)(2,1)} copy(bf16[640,128]{1,0:T(8,128)(2,1)} %get-tuple-element.13) | data formatting | bytes 327680
